TPU v7x, 32 devices: a 4x2x2 block of a 4x4x8 slice. The times are simulated.
32 devices in a mesh: dp: 4 (over y, z), tp: 8 (over x, core).
Axes of the slice: x: 4, y: 2, z: 2, core: 2. Of those that a mesh axis runs over, the one named last changes fastest.
The devices are a block of a 4x4x8 slice.
Arguments:
- x: bfloat16 [12288, 2048], P(('dp', 'tp')), parts along dimension 0
- dy: bfloat16 [12288, 2048], P(('dp', 'tp')), parts along dimension 0
- wg: bfloat16 [2048, 8192], P(None, 'tp')
- wu: bfloat16 [2048, 8192], P(None, 'tp')
- wd: bfloat16 [8192, 2048], P('tp')
- ug: bfloat16 [12288, 8192], P('dp', 'tp'), parts along dimension 0
- uu: bfloat16 [12288, 8192], P('dp', 'tp'), parts along dimension 0
Outputs:
- output 1: bfloat16 [12288, 2048], P(('dp', 'tp')), parts along dimension 0
- output 2: float32 [8192, 8192], P('dp', 'tp'), parts along dimension 0
- output 3: float32 [8192, 8192], P('dp', 'tp'), parts along dimension 0
- output 4: float32 [32768, 2048], P(('dp', 'tp')), parts along dimension 0
There are 4 independent parts. A program takes and returns all parts, laid end to end along the dimension named above; an argument that names none is the same for every part.
All inputs are finite; a program needn't handle non-finite values.
Results may differ from a plain program's by a relative error of at most 0.0130648.
Values are sent between devices in bfloat16 or wider.
A program may use at most 768 MiB of HBM per device.

v0:
```python
import jax
import jax.numpy as jnp
from jax import lax
from jax.sharding import PartitionSpec as P


def solution(mesh):
    tok = P(("dp", "tp"), None)
    col = P(None, "tp")
    row = P("tp", None)
    act = P("dp", "tp")

    def body(x, dy, wg, wu, wd, ug, uu):
        xg = lax.all_gather(x, "tp", axis=0, tiled=True)
        dyg = lax.all_gather(dy, "tp", axis=0, tiled=True)
        ug32 = ug.astype(jnp.float32)
        uu32 = uu.astype(jnp.float32)
        s = jax.nn.sigmoid(ug32)
        a = ug32 * s
        z = (a * uu32).astype(jnp.bfloat16)
        dwd = jnp.dot(z.T, dyg, preferred_element_type=jnp.float32)
        g = jnp.dot(dyg, wd.T, preferred_element_type=jnp.float32)
        duu = (g * a).astype(jnp.bfloat16)
        dug = (g * uu32 * s * (1.0 + ug32 * (1.0 - s))).astype(jnp.bfloat16)
        p = jnp.dot(dug, wg.T, preferred_element_type=jnp.float32) + jnp.dot(duu, wu.T, preferred_element_type=jnp.float32)
        dx = lax.psum_scatter(p.astype(jnp.bfloat16), "tp", scatter_dimension=0, tiled=True)
        dwg = jnp.dot(xg.T, dug, preferred_element_type=jnp.float32)
        dwu = jnp.dot(xg.T, duu, preferred_element_type=jnp.float32)
        return dx, dwg, dwu, dwd

    return jax.shard_map(body, mesh=mesh, in_specs=(tok, tok, col, col, row, act, act), out_specs=(tok, act, act, tok), check_vma=False)
```

profile of v0, /device:TPU:81, one launch (start us, length us, event | category | flops | bytes accessed | tf_op | source)
XLA Modules:
  0.0 244.6 jit_solution(8522522197410454193)
XLA Ops:
  7.2 0.1 all-gather.3.cloned.1.call-start
  7.2 0.7 all-gather.3.cloned.1.call-update
  8.0 0.1 all-gather.5.cloned.1.call-start
  8.0 0.7 all-gather.5.cloned.1.call-update
  8.8 0.1 reduce-scatter.2.cloned.1.call-start
  8.9 69.5 %all-gather.3.cloned.1.call-done = bf16[3072,2048]{1,0:T(8,128)(2,1)} async-done(((bf16[384,2048]{1,0:T(8,128)(2,1)}), bf16[3072,2048]{1,0:T(8,128)(2,1)}) %all-gather.3.cloned.1.call-update) | async-done | bytes 12582928 | tf_op jit(solution)/shard_map/all_gather | solution.py:15
  78.4 29.6 %fusion.2 = (bf16[3072,1024]{1,0:T(8,128)(2,1)}, f32[3072,1024]{1,0:T(8,128)}) fusion(bf16[3072,1024]{1,0:T(8,128)(2,1)} %param.13, bf16[3072,1024]{1,0:T(8,128)(2,1)} %param.12, bf16[3072,2048]{1,0:T(8,128)(2,1)} %all-gather.3.cloned.1.call-done, bf16[1024,2048]{1,0:T(8,128)(2,1)} %param.11), kind=kOutput, calls=%fused_computation.8 | convolution fusion | flops 12922650624 | bytes 48234496 | tf_op jit(solution)/shard_map/dot_general | solution.py:22
  108.0 19.9 %fusion.11 = f32[3072,2048]{1,0:T(8,128)} fusion(bf16[3072,1024]{1,0:T(8,128)(2,1)} %get-tuple-element.8, bf16[2048,1024]{1,0:T(8,128)(2,1)} %param.9), kind=kOutput, calls=%fused_computation.19 | convolution fusion | flops 12884901888 | bytes 35651584 | tf_op jit(solution)/shard_map/dot_general | solution.py:25
  127.9 27.0 %add_convert_fusion = bf16[3072,2048]{1,0:T(8,128)(2,1)} fusion(f32[3072,2048]{1,0:T(8,128)} %fusion.11, bf16[2048,1024]{1,0:T(8,128)(2,1)} %param.10, f32[3072,1024]{1,0:T(8,128)} %get-tuple-element.9, bf16[3072,1024]{1,0:T(8,128)(2,1)} %param.12), kind=kOutput, calls=%fused_computation | convolution fusion | flops 12919504896 | bytes 60817408 | tf_op jit(solution)/shard_map/dot_general | solution.py:25
  154.9 0.1 reduce-scatter.2.cloned.1.call-update
  155.0 0.0 all-gather.5.cloned.1.call-done
  155.0 18.9 %convolution_bitcast_fusion.1 = f32[2048,1024]{0,1:T(8,128)} fusion(bf16[3072,1024]{1,0:T(8,128)(2,1)} %get-tuple-element.8, bf16[3072,2048]{1,0:T(8,128)(2,1)} %all-gather.5.cloned.1.call-done), kind=kOutput, calls=%fused_computation.17 | convolution fusion | flops 12884901888 | bytes 27262976 | tf_op jit(solution)/shard_map/dot_general | solution.py:27
  173.9 9.3 %copy.11 = f32[2048,1024]{1,0:T(8,128)} copy(f32[2048,1024]{0,1:T(8,128)} %convolution_bitcast_fusion.1) | data formatting | bytes 16777216
  183.3 23.7 %convolution_bitcast_fusion = f32[2048,1024]{0,1:T(8,128)} fusion(bf16[3072,2048]{1,0:T(8,128)(2,1)} %all-gather.5.cloned.1.call-done, f32[3072,1024]{1,0:T(8,128)} %get-tuple-element.9, bf16[3072,1024]{1,0:T(8,128)(2,1)} %param.12), kind=kOutput, calls=%fused_computation.16 | convolution fusion | flops 12906921984 | bytes 39845888 | tf_op jit(solution)/shard_map/dot_general | solution.py:28
  207.0 9.3 %copy.12 = f32[2048,1024]{1,0:T(8,128)} copy(f32[2048,1024]{0,1:T(8,128)} %convolution_bitcast_fusion) | data formatting | bytes 16777216
  216.3 21.8 %fusion.8 = f32[1024,2048]{1,0:T(8,128)} fusion(bf16[3072,2048]{1,0:T(8,128)(2,1)} %all-gather.3.cloned.1.call-done, bf16[3072,1024]{1,0:T(8,128)(2,1)} %param.13, bf16[3072,1024]{1,0:T(8,128)(2,1)} %param.12), kind=kOutput, calls=%fused_computation.15 | convolution fusion | flops 12910067712 | bytes 33554432 | tf_op jit(solution)/shard_map/dot_general | solution.py:21
  238.0 0.0 reduce-scatter.2.cloned.1.call-done
Async XLA Ops:
  7.2 71.2 %all-gather.3.cloned.1.call-start = ((), (), s32[]{:S(2)}) async-start(), calls=%async_computation.1 | async-start | bytes 14155776 | tf_op jit(solution)/shard_map/all_gather | solution.py:15
  8.0 147.1 %all-gather.5.cloned.1.call-start = ((), (), s32[]{:S(2)}) async-start(), calls=%async_computation.3 | async-start | bytes 14155776 | tf_op jit(solution)/shard_map/all_gather | solution.py:14
  8.8 229.2 %reduce-scatter.2.cloned.1.call-start = ((), (), s32[]{:S(2)}) async-start(), calls=%async_computation.2 | async-start | bytes 14155776 | tf_op jit(solution)/shard_map/reduce_scatter | solution.py:26
Sparse Core Ops, SparseCore 0:
  9.6 68.7 all-gather.2
  80.0 64.5 all-gather.4
  155.1 68.3 reduce-scatter.1
where the time goes:
time: 245 us
  matrix products  141 us (58%)
  waiting for transfers between devices  71.1 us (29%)
  local copies, waits for them, and re-layouts  18.6 us (8%)
  between operations  13.8 us (6%)
    all_gather x1, waiting for transfers between devices, body(): dyg = lax.all_gather(dy, 'tp', axis=0, tiled=True)  69.5 us
    dot_general x1, matrix products, body(): g = jnp.dot(dyg, wd.T, preferred_element_type=jnp.float32)  29.6 us
    dot_general x1, matrix products, body(): jnp.dot(duu, wu.T, preferred_element_type=jnp.float32)  27 us
    dot_general x1, matrix products, body(): dwu = jnp.dot(xg.T, duu, preferred_element_type=jnp.float32)  23.7 us
    dot_general x1, matrix products, body(): dwd = jnp.dot(z.T, dyg, preferred_element_type=jnp.float32)  21.8 us
    dot_general x1, matrix products, body(): jnp.dot(dug, wg.T, preferred_element_type=jnp.float32)  19.9 us
    dot_general x1, matrix products, body(): dwg = jnp.dot(xg.T, dug, preferred_element_type=jnp.float32)  18.9 us
    unnamed x2, local copies, waits for them, and re-layouts  18.6 us
  transfers between devices with their start and end apart: 3, of which 1 were waited for; matrix products, arithmetic and copies ran while one was open for 65% of the time, Pallas kernels for 0%

commit v1 on v0

v1 whole, which is shorter than its diff:
```python
import functools

import jax
import jax.numpy as jnp
from jax import lax
from jax.experimental import pallas as pl
from jax.experimental.pallas import tpu as pltpu
from jax.sharding import PartitionSpec as P


MESH = pl.DeviceIdType.MESH
BF = jnp.bfloat16
F32 = jnp.float32
NT = (((1,), (1,)), ((), ()))
TN = (((0,), (0,)), ((), ()))

R_A, R_B, L_A, L_B, F_R, F_L, Q_OWN, Q_LA, Q_LB, Q_RA, Q_RB, Q_OA, Q_OB = range(13)


def gather_kernel(
    n, x, dy, wd, wg, wu, ug, uu,
    xg, dyg, dug, duu, dwd, s_own, s_la, s_lb, s_ra, s_rb, s_oa, s_ob, pbuf, rbuf,
    vwd, vwg, vwu, vdy, vug, vuu, vdug, vduu, vz, vp, vq, vdw,
    ss, rs, sx, rx, wsem, usem, dsem, osem, psem, qsem,
):
    rows, hid = x.shape
    half = rows // 2
    ff = wd.shape[0]
    me = lax.axis_index("tp")
    core = lax.rem(me, 2)
    right, left = lax.rem(me + 2, n), lax.rem(me + n - 2, n)
    opp = lax.rem(me + 4, n)
    mate = me + 1 - 2 * core

    def whole(d):
        return pl.ds(pl.multiple_of(d * rows, rows), rows)

    def part(d, h):
        return pl.ds(pl.multiple_of(d * rows + h * half, half), half)

    def at(slot):
        return pl.ds(slot * rows, rows)

    def mate_of(d):
        return d + 1 - 2 * core

    def remote(src, dst, k, i, dev):
        return pltpu.make_async_remote_copy(
            src, dst, ss.at[k, i], rs.at[k, i], device_id={"tp": dev}, device_id_type=MESH
        )

    gathers = ((dy, dyg), (x, xg))

    def send_own(k):
        src, dst = gathers[k]
        a, b = pl.ds(0, half), pl.ds(half, half)
        remote(src.at[a], dst.at[part(me, 0)], k, R_A, right).start()
        remote(src.at[b], dst.at[part(me, 1)], k, L_B, left).start()
        remote(src, dst.at[whole(me)], k, Q_OWN, mate).start()
        remote(src.at[b], dst.at[part(me, 1)], k, R_B, right).start()
        remote(src.at[a], dst.at[part(me, 0)], k, L_A, left).start()

    def piece(k, d, h, i, dev):
        dst = gathers[k][1]
        return remote(dst.at[part(d, h)], dst.at[part(d, h)], k, i, dev)

    def relay_first(k):
        piece(k, left, 0, R_A, right).wait_recv()
        piece(k, left, 0, F_R, right).start()
        piece(k, left, 0, Q_LA, mate).start()
        piece(k, right, 1, L_B, left).wait_recv()
        piece(k, right, 1, F_L, left).start()
        piece(k, right, 1, Q_RB, mate).start()

    def relay_second(k):
        piece(k, left, 1, R_B, right).wait_recv()
        piece(k, left, 1, Q_LB, mate).start()
        piece(k, right, 0, L_A, left).wait_recv()
        piece(k, right, 0, Q_RA, mate).start()

    def relay_third(k):
        piece(k, opp, 0, F_R, right).wait_recv()
        piece(k, opp, 0, Q_OA, mate).start()
        piece(k, opp, 1, F_L, left).wait_recv()
        piece(k, opp, 1, Q_OB, mate).start()

    def drain(k):
        src, dst = gathers[k]
        for i in (R_A, R_B, L_A, L_B, F_R, F_L, Q_LA, Q_LB, Q_RA, Q_RB, Q_OA, Q_OB):
            piece(k, me, 0, i, right).wait_send()
        remote(src, dst.at[whole(me)], k, Q_OWN, mate).wait_send()

    def wait_mate(k, *slots):
        for i in slots:
            piece(k, me, 0, i, mate).wait_recv()

    barrier = pltpu.get_barrier_semaphore()
    for dev in (right, left, mate):
        pl.semaphore_signal(barrier, inc=1, device_id={"tp": dev}, device_id_type=MESH)
    pl.semaphore_wait(barrier, 3)

    send_own(0)
    loads = [pltpu.make_async_copy(a, b, wsem.at[i]) for i, (a, b) in enumerate(((wd, vwd), (wg, vwg), (wu, vwu)))]
    for c in loads:
        c.start()

    def u_load(d, slot):
        return (
            pltpu.make_async_copy(ug.at[whole(d)], vug.at[slot], usem.at[0, slot]),
            pltpu.make_async_copy(uu.at[whole(d)], vuu.at[slot], usem.at[1, slot]),
        )

    def outs(d, slot):
        return (
            pltpu.make_async_copy(vdug.at[slot], dug.at[whole(d)], osem.at[0, slot]),
            pltpu.make_async_copy(vduu.at[slot], duu.at[whole(d)], osem.at[1, slot]),
        )

    def p_out(slot, j):
        if slot == 0:
            return (pltpu.make_async_copy(vp.at[0], pbuf.at[j], psem.at[0]),)
        if j == 0:
            return (pltpu.make_async_copy(vp.at[1], s_own, psem.at[1]),)
        a, b = ((s_la, s_lb), (s_ra, s_rb), (s_oa, s_ob))[j - 1]
        return (
            pltpu.make_async_copy(vp.at[1, pl.ds(0, half)], a, psem.at[1]),
            pltpu.make_async_copy(vp.at[1, pl.ds(half, half)], b, psem.at[2]),
        )

    def swap(j):
        return pltpu.make_async_remote_copy(
            pbuf.at[j], rbuf.at[j], sx.at[j], rx.at[j], device_id={"tp": mate}, device_id_type=MESH
        )

    chips = (me, left, right, opp)
    order = [(j, slot, mate_of(chips[j]) if slot == 0 else chips[j]) for j in range(4) for slot in (0, 1)]

    for c in u_load(order[0][2], 0):
        c.start()
    own_x = (pltpu.make_async_copy(x, vq, qsem.at[1]), pltpu.make_async_copy(vq, xg.at[whole(me)], qsem.at[1]))
    own_dy = (pltpu.make_async_copy(dy, vdy.at[at(1)], dsem.at[1]), pltpu.make_async_copy(vdy.at[at(1)], dyg.at[whole(me)], qsem.at[2]))
    own_x[0].start()
    own_dy[0].start()
    own_x[0].wait()
    own_x[1].start()
    own_dy[0].wait()
    own_dy[1].start()
    own_x[1].wait()

    gn = min(256, ff)
    hn = min(512, hid)

    def block(step):
        j, slot, d = order[step]
        if step != 1:
            load = pltpu.make_async_copy(dyg.at[whole(d)], vdy.at[at(slot)], dsem.at[slot])
            load.start()
            load.wait()
        for c in u_load(d, slot):
            c.wait()
        if step + 1 < 8:
            for c in u_load(order[step + 1][2], 1 - slot):
                c.start()
        if step >= 2:
            for c in outs(d, slot):
                c.wait()
        if slot == 1:
            for c in p_out(0, j):
                c.wait()
            swap(j).start()

        @pl.loop(0, ff // gn)
        def _(i):
            cols = pl.ds(pl.multiple_of(i * gn, gn), gn)
            g = lax.dot_general(vdy[at(slot), :], vwd[cols, :], NT, preferred_element_type=F32)
            u = vug[slot, :, cols].astype(F32)
            v = vuu[slot, :, cols].astype(F32)
            s = jax.nn.sigmoid(u)
            a = u * s
            vz[at(slot), cols] = (a * v).astype(BF)
            vduu[slot, :, cols] = (g * a).astype(BF)
            vdug[slot, :, cols] = (g * v * s * (1.0 + u * (1.0 - s))).astype(BF)

        for c in outs(d, slot):
            c.start()
        if slot == 1:
            swap(j).wait_recv()
            got = pltpu.make_async_copy(rbuf.at[j], vq, qsem.at[0])
            got.start()
            got.wait()
            if j > 0:
                for c in p_out(1, j - 1):
                    c.wait()

        @pl.loop(0, hid // hn)
        def _(i):
            cols = pl.ds(pl.multiple_of(i * hn, hn), hn)
            p = lax.dot_general(vdug[slot], vwg[cols, :], NT, preferred_element_type=F32)
            p += lax.dot_general(vduu[slot], vwu[cols, :], NT, preferred_element_type=F32)
            if slot == 1:
                p += vq[:, cols].astype(F32)
            vp[slot, :, cols] = p.astype(BF)

        for c in p_out(slot, j):
            c.start()
        if slot == 1:
            nt = min(512, hid)

            @pl.loop(0, ff // gn)
            def _(i):
                mine = pl.ds(pl.multiple_of(i * gn, gn), gn)
                zt = vz[:, mine]
                for k in range(0, hid, nt):
                    part_sum = lax.dot_general(zt, vdy[:, k : k + nt], TN, preferred_element_type=F32)
                    if j == 0:
                        vdw[mine, k : k + nt] = part_sum
                    else:
                        vdw[mine, k : k + nt] += part_sum

    remote(dy, dyg.at[whole(me)], 0, Q_OWN, mate).wait_recv()
    for c in loads:
        c.wait()
    block(0)
    block(1)
    own_dy[1].wait()
    relay_first(0)
    send_own(1)
    relay_second(0)
    wait_mate(0, Q_LA, Q_LB)
    block(2)
    block(3)
    wait_mate(0, Q_RA, Q_RB)
    relay_third(0)
    block(4)
    block(5)
    wait_mate(0, Q_OA, Q_OB)
    relay_first(1)
    block(6)
    block(7)
    dw_out = pltpu.make_async_copy(vdw, dwd, qsem.at[1])
    dw_out.start()
    relay_second(1)
    for step in (6, 7):
        j, slot, d = order[step]
        for c in outs(d, slot):
            c.wait()
    for c in p_out(1, 3):
        c.wait()
    for j in range(4):
        swap(j).wait_send()
    relay_third(1)
    dw_out.wait()
    remote(x, xg.at[whole(me)], 1, Q_OWN, mate).wait_recv()
    wait_mate(1, Q_LA, Q_LB, Q_RA, Q_RB, Q_OA, Q_OB)
    drain(0)
    drain(1)


def gather_and_local(n, x, dy, wd, wg, wu, ug, uu):
    rows, hid = x.shape
    tok, ff = ug.shape
    half = rows // 2
    any_ = pl.BlockSpec(memory_space=pl.ANY)
    sds = jax.ShapeDtypeStruct
    out = [sds((tok, hid), BF)] * 2 + [sds((tok, ff), BF)] * 2 + [sds((ff, hid), F32), sds((rows, hid), BF)] + [sds((half, hid), BF)] * 6
    out += [sds((n // 2, rows, hid), BF)] * 2
    return pl.pallas_call(
        functools.partial(gather_kernel, n),
        out_shape=out,
        in_specs=[any_] * 7,
        out_specs=[any_] * len(out),
        scratch_shapes=[
            pltpu.VMEM(wd.shape, BF), pltpu.VMEM(wg.shape, BF), pltpu.VMEM(wu.shape, BF),
            pltpu.VMEM((2 * rows, hid), BF),
            pltpu.VMEM((2, rows, ff), BF), pltpu.VMEM((2, rows, ff), BF),
            pltpu.VMEM((2, rows, ff), BF), pltpu.VMEM((2, rows, ff), BF), pltpu.VMEM((2 * rows, ff), BF),
            pltpu.VMEM((2, rows, hid), BF),
            pltpu.VMEM((rows, hid), BF),
            pltpu.VMEM((ff, hid), F32),
            pltpu.SemaphoreType.DMA((2, 13)), pltpu.SemaphoreType.DMA((2, 13)),
            pltpu.SemaphoreType.DMA((4,)), pltpu.SemaphoreType.DMA((4,)),
            pltpu.SemaphoreType.DMA((3,)), pltpu.SemaphoreType.DMA((2, 2)), pltpu.SemaphoreType.DMA((2,)),
            pltpu.SemaphoreType.DMA((2, 2)), pltpu.SemaphoreType.DMA((3,)), pltpu.SemaphoreType.DMA((3,)),
        ],
        compiler_params=pltpu.CompilerParams(collective_id=0, has_side_effects=True, vmem_limit_bytes=60 * 2**20),
        cost_estimate=pl.CostEstimate(flops=8 * tok * hid * ff, bytes_accessed=100 * 2**20, transcendentals=tok * ff),
    )(x, dy, wd, wg, wu, ug, uu)


def tokens_kernel(kt, a, b, o, vb, sem):
    tok = a.shape[0]
    copies = [
        pltpu.make_async_copy(b.at[pl.ds(k, kt)], vb.at[pl.ds(k, kt)], sem.at[k // kt]) for k in range(0, tok, kt)
    ]

    @pl.when(pl.program_id(0) == 0)
    def _():
        for c in copies:
            c.start()
        for i, c in enumerate(copies):
            c.wait()
            ks = pl.ds(i * kt, kt)
            p = lax.dot_general(a[ks, :], vb[ks, :], TN, preferred_element_type=F32)
            if i == 0:
                o[...] = p
            else:
                o[...] += p

    @pl.when(pl.program_id(0) > 0)
    def _():
        o[...] = lax.dot_general(a[...], vb[...], TN, preferred_element_type=F32)


def over_tokens(a, b, m_tile=256, kt=768):
    tok, m = a.shape
    k = b.shape[1]
    m_tile, kt = min(m_tile, m), min(kt, tok)
    return pl.pallas_call(
        functools.partial(tokens_kernel, kt),
        grid=(m // m_tile,),
        out_shape=jax.ShapeDtypeStruct((m, k), F32),
        in_specs=[pl.BlockSpec((tok, m_tile), lambda i: (0, i)), pl.BlockSpec(memory_space=pl.ANY)],
        out_specs=pl.BlockSpec((m_tile, k), lambda i: (i, 0)),
        scratch_shapes=[pltpu.VMEM((tok, k), BF), pltpu.SemaphoreType.DMA((tok // kt,))],
        compiler_params=pltpu.CompilerParams(vmem_limit_bytes=62 * 2**20),
        cost_estimate=pl.CostEstimate(
            flops=2 * tok * m * k, bytes_accessed=2 * tok * (m + k) + 4 * m * k, transcendentals=0
        ),
    )(a, b)


def sum_kernel(*refs):
    for i, group in enumerate((refs[1:3], refs[3:5])):
        total = refs[0][i].astype(F32)
        for r in group:
            total += r[...].astype(F32)
        refs[-1][i] = total.astype(BF)


def final_sum(own, a_terms, b_terms, steps=4):
    rows, hid = own.shape
    half = rows // 2
    t = half // steps
    both = pl.BlockSpec((2, t, hid), lambda i: (0, i, 0))
    one = pl.BlockSpec((t, hid), lambda i: (i, 0))
    return pl.pallas_call(
        sum_kernel,
        grid=(steps,),
        out_shape=jax.ShapeDtypeStruct((2, half, hid), BF),
        in_specs=[both] + [one] * 4,
        out_specs=both,
        compiler_params=pltpu.CompilerParams(vmem_limit_bytes=16 * 2**20),
        cost_estimate=pl.CostEstimate(flops=rows * hid * 3, bytes_accessed=8 * rows * hid, transcendentals=0),
    )(own.reshape(2, half, hid), *a_terms, *b_terms).reshape(rows, hid)


def solution(mesh):
    tok = P(("dp", "tp"), None)
    col = P(None, "tp")
    row = P("tp", None)
    act = P("dp", "tp")
    n = mesh.shape["tp"]
    to_right = [(i, (i + 2) % n) for i in range(n)]
    to_left = [(i, (i - 2) % n) for i in range(n)]

    def add(*terms):
        return functools.reduce(jnp.add, [t.astype(F32) for t in terms]).astype(BF)

    def body(x, dy, wg, wu, wd, ug, uu):
        xg, _, dug, duu, dwd, s_own, s_la, s_lb, s_ra, s_rb, s_oa, s_ob, _, _ = gather_and_local(
            n, x, dy, wd, wg, wu, ug, uu
        )

        def right(v):
            return lax.ppermute(v, "tp", to_right)

        def left(v):
            return lax.ppermute(v, "tp", to_left)

        from_right = left(s_oa)
        from_left = right(s_ob)
        direct_a = right(s_ra)
        direct_b = left(s_lb)
        dwg = over_tokens(xg, dug)
        from_right, from_left, dwg = lax.optimization_barrier((from_right, from_left, dwg))
        next_l = add(s_la, from_right)
        next_r = add(s_rb, from_left)
        next_l, next_r, xg = lax.optimization_barrier((next_l, next_r, xg))
        relay_a = left(next_l)
        relay_b = right(next_r)
        dwu = over_tokens(xg, duu)
        dx = final_sum(s_own, (direct_a, relay_a), (direct_b, relay_b))
        return dx, dwg, dwu, dwd

    return jax.shard_map(
        body, mesh=mesh, in_specs=(tok, tok, col, col, row, act, act), out_specs=(tok, act, act, tok), check_vma=False
    )
```

time: 245 us -> 192 us (0.78)
  Pallas kernels: 0 us -> 159 us
  matrix products: 141 us -> 0 us
  waiting for transfers between devices: 71.1 us -> 13 us
  between operations: 13.8 us -> 0.71 us
  local copies, waits for them, and re-layouts: 18.6 us -> 7.9 us
  starting transfers between devices: 0.18 us -> 6.91 us
  other arithmetic: 0 us -> 3.18 us
    pallas_call x0 -> x4, Pallas kernels: none -> 159 us  [the longest x1 117 us: gather_and_local(): pl.pallas_call(functools.partial(gather_kernel, n), out_shape=out, in_spe...]
    dot_general x6 -> x0, matrix products: 141 us -> none  [the longest x1 29.6 us: body(): g = jnp.dot(dyg, wd.T, preferred_element_type=jnp.float32)]
    all_gather x2 -> x0, waiting for transfers between devices: 69.6 us -> none  [the longest x1 69.5 us: body(): dyg = lax.all_gather(dy, 'tp', axis=0, tiled=True)]
    ppermute x0 -> x6, waiting for transfers between devices: none -> 13 us  [the longest x3 13 us: right(): return lax.ppermute(v, 'tp', to_right)]
    unnamed x2 -> x7, local copies, waits for them, and re-layouts: 18.6 us -> 7.9 us
    ppermute x0 -> x6, starting transfers between devices: none -> 6.91 us  [the longest x3 4.33 us: left(): return lax.ppermute(v, 'tp', to_left)]
    convert_element_type x0 -> x1, other arithmetic: none -> 3.18 us  [add(): return functools.reduce(jnp.add, [t.astype(F32) for t in terms]).astype(BF)]
  transfers between devices with their start and end apart: 3 -> 6, of which waited for: 1 -> 1; matrix products, arithmetic and copies ran while one was open for 65% -> 2% of each run, Pallas kernels for 0% -> 20%
where the time goes in v1:
time: 192 us; the launch traced here: 191 us
  Pallas kernels  159 us (83%)
  waiting for transfers between devices  13 us (7%)
  local copies, waits for them, and re-layouts  7.9 us (4%)
  starting transfers between devices  6.91 us (4%)
  other arithmetic  3.18 us (2%)
    pallas_call x1, Pallas kernels, gather_and_local(): pl.pallas_call(functools.partial(gather_kernel, n), out_shape=out, in_spe...  117 us
    pallas_call x2, Pallas kernels, over_tokens(): pl.pallas_call(functools.partial(tokens_kernel, kt), grid=(m // m_tile,),...  37.9 us
    ppermute x3, waiting for transfers between devices, right(): return lax.ppermute(v, 'tp', to_right)  13 us
    unnamed x7, local copies, waits for them, and re-layouts  7.9 us
    ppermute x3, starting transfers between devices, left(): return lax.ppermute(v, 'tp', to_left)  4.33 us
    pallas_call x1, Pallas kernels, final_sum(): pl.pallas_call(sum_kernel, grid=(steps,), out_shape=jax.ShapeDtypeStruct(...  4.25 us
  transfers between devices with their start and end apart: 6, of which 1 were waited for; matrix products, arithmetic and copies ran while one was open for 2% of the time, Pallas kernels for 20%

profile of v1, /device:TPU:81, one launch (start us, length us, event | category | flops | bytes accessed | tf_op | source)
XLA Modules:
  0.0 190.7 jit_solution(4666708220976550260)
XLA Ops:
  0.6 116.8 %shard_map.102 = (bf16[3072,2048]{1,0:T(8,128)(2,1)}, bf16[3072,2048]{1,0:T(8,128)(2,1)}, bf16[3072,1024]{1,0:T(8,128)(2,1)}, bf16[3072,1024]{1,0:T(8,128)(2,1)}...) custom-call(bf16[384,2048]{1,0:T(8,128)(2,1)} %x.1, ...), custom_call_target="tpu_custom_call" | custom-call | flops 51539607552 | bytes 104857600 | tf_op jit(solution)/shard_map/pallas_call | solution.py:267
  117.4 1.1 collective-permute-start
  118.5 1.7 collective-permute-start.1
  120.2 0.0 collective-permute-start.2
  120.2 2.7 %collective-permute-start.4 = (bf16[192,2048]{1,0:T(8,128)(2,1)}, bf16[192,2048]{1,0:T(8,128)(2,1)}, u32[]{:S(2)}, u32[]{:S(2)}) collective-permute-start(bf16[192,2048]{1,0:T(8,128)(2,1)} %get-tuple-element.32), channel_id=1, source_target_pairs={{0,6},{1,7},{2,0},{3,1},{4,2},{5,3},{6,4},{7,5},{8,14},{9,15},{10,... | collective-permute-start | bytes 2359304 | tf_op jit(solution)/shard_map/ppermute | solution.py:378
  122.9 0.0 copy-start.1
  122.9 0.0 copy-start.2
  122.9 19.0 %shard_map.103 = f32[2048,1024]{1,0:T(8,128)} custom-call(bf16[3072,2048]{1,0:T(8,128)(2,1)} %get-tuple-element.35.a, bf16[3072,1024]{1,0:T(8,128)(2,1)} %get-tuple-element.27.b), custom_call_target="tpu_custom_call" | custom-call | flops 12884901888 | bytes 27262976 | tf_op jit(solution)/shard_map/pallas_call | solution.py:318
  141.8 0.0 collective-permute-done.1
  141.8 13.0 %collective-permute-done.2 = bf16[192,2048]{1,0:T(8,128)(2,1)} collective-permute-done((bf16[192,2048]{1,0:T(8,128)(2,1)}, bf16[192,2048]{1,0:T(8,128)(2,1)}, u32[]{:S(2)}, u32[]{:S(2)}) %collective-permute-start.2) | collective-permute-done | bytes 786464 | tf_op jit(solution)/shard_map/ppermute | solution.py:375
  154.9 0.0 copy-done.1
  154.9 0.0 copy-done.2
  154.9 3.2 %add_convert_fusion = (bf16[192,2048]{1,0:T(8,128)(2,1)}, bf16[192,2048]{1,0:T(8,128)(2,1)}) fusion(bf16[192,2048]{1,0:T(8,128)(2,1)} %collective-permute-done.2, bf16[192,2048]{1,0:T(8,128)(2,1)S(1)} %copy-done.2, bf16[192,2048]{1,0:T(8,128)(2,1)} %collective-permute-done.1, bf16[192,2048]{1,0:T(8,128)(2,1)S(1)} %copy-done.1), kind=kLoop, calls=%fused_computation | loop fusion | flops 3145728 | bytes 4718592 | tf_op jit(solution)/shard_map/convert_element_type | solution.py:367
  158.1 0.0 collective-permute-start.3
  158.1 1.5 collective-permute-start.5
  159.5 0.0 copy-start
  159.5 19.0 %shard_map.105 = f32[2048,1024]{1,0:T(8,128)} custom-call(bf16[3072,2048]{1,0:T(8,128)(2,1)} %get-tuple-element.35.a, bf16[3072,1024]{1,0:T(8,128)(2,1)} %get-tuple-element.36.b), custom_call_target="tpu_custom_call" | custom-call | flops 12884901888 | bytes 27262976 | tf_op jit(solution)/shard_map/pallas_call | solution.py:318
  178.5 0.0 collective-permute-done.refs_1_
  178.5 0.0 collective-permute-done.4.refs_3_
  178.5 0.0 collective-permute-done.3.refs_2_
  178.5 0.0 collective-permute-done.5.refs_4_
  178.6 0.0 copy-done
  178.6 4.2 %shard_map.104 = bf16[2,192,2048]{2,1,0:T(8,128)(2,1)} custom-call(bf16[2,192,2048]{2,1,0:T(8,128)(2,1)S(1)} %bitcast.2, bf16[192,2048]{1,0:T(8,128)(2,1)} %collective-permute-done.refs_1_, bf16[192,2048]{1,0:T(8,128)(2,1)} %collective-permute-done.3.refs_2_, bf16[192,2048]{1,0:T(8,128)(2,1)} %collective-permute-done.4.refs_3_, ...), custom_call_target="tpu_custom_call" | custom-call | flops 2359296 | bytes 6291456 | tf_op jit(solution)/shard_map/pallas_call | solution.py:346
  182.8 7.9 %copy.12 = f32[1024,2048]{1,0:T(8,128)} copy(f32[1024,2048]{1,0:T(8,128)} %get-tuple-element.47) | data formatting | bytes 16777216
Async XLA Ops:
  117.4 61.1 %collective-permute-start = (bf16[192,2048]{1,0:T(8,128)(2,1)}, bf16[192,2048]{1,0:T(8,128)(2,1)}, u32[]{:S(2)}, u32[]{:S(2)}) collective-permute-start(bf16[192,2048]{1,0:T(8,128)(2,1)} %get-tuple-element.22), channel_id=1, source_target_pairs={{0,2},{1,3},{2,4},{3,5},{4,6},{5,7},{6,0},{7,1},{8,10},{9,11},{10,... | collective-permute-start | bytes 2359304 | tf_op jit(solution)/shard_map/ppermute | solution.py:375
  118.5 23.3 %collective-permute-start.1 = (bf16[192,2048]{1,0:T(8,128)(2,1)}, bf16[192,2048]{1,0:T(8,128)(2,1)}, u32[]{:S(2)}, u32[]{:S(2)}) collective-permute-start(bf16[192,2048]{1,0:T(8,128)(2,1)} %get-tuple-element.24), channel_id=1, source_target_pairs={{0,6},{1,7},{2,0},{3,1},{4,2},{5,3},{6,4},{7,5},{8,14},{9,15},{10,... | collective-permute-start | bytes 2359304 | tf_op jit(solution)/shard_map/ppermute | solution.py:378
  120.2 34.7 %collective-permute-start.2 = (bf16[192,2048]{1,0:T(8,128)(2,1)}, bf16[192,2048]{1,0:T(8,128)(2,1)}, u32[]{:S(2)}, u32[]{:S(2)}) collective-permute-start(bf16[192,2048]{1,0:T(8,128)(2,1)} %get-tuple-element.25), channel_id=1, source_target_pairs={{0,2},{1,3},{2,4},{3,5},{4,6},{5,7},{6,0},{7,1},{8,10},{9,11},{10,... | collective-permute-start | bytes 2359304 | tf_op jit(solution)/shard_map/ppermute | solution.py:375
  120.2 58.3 %collective-permute-start.4 = (bf16[192,2048]{1,0:T(8,128)(2,1)}, bf16[192,2048]{1,0:T(8,128)(2,1)}, u32[]{:S(2)}, u32[]{:S(2)}) collective-permute-start(bf16[192,2048]{1,0:T(8,128)(2,1)} %get-tuple-element.32), channel_id=1, source_target_pairs={{0,6},{1,7},{2,0},{3,1},{4,2},{5,3},{6,4},{7,5},{8,14},{9,15},{10,... | collective-permute-start | bytes 2359304 | tf_op jit(solution)/shard_map/ppermute | solution.py:378
  122.9 32.0 %copy-start.1 = (bf16[192,2048]{1,0:T(8,128)(2,1)S(1)}, bf16[192,2048]{1,0:T(8,128)(2,1)}, u32[]{:S(2)}) copy-start(bf16[192,2048]{1,0:T(8,128)(2,1)} %get-tuple-element.23) | copy-start | bytes 2359300
  122.9 32.0 %copy-start.2 = (bf16[192,2048]{1,0:T(8,128)(2,1)S(1)}, bf16[192,2048]{1,0:T(8,128)(2,1)}, u32[]{:S(2)}) copy-start(bf16[192,2048]{1,0:T(8,128)(2,1)} %get-tuple-element.29) | copy-start | bytes 2359300
  158.1 20.5 %collective-permute-start.3 = (bf16[192,2048]{1,0:T(8,128)(2,1)}, bf16[192,2048]{1,0:T(8,128)(2,1)}, u32[]{:S(2)}, u32[]{:S(2)}) collective-permute-start(bf16[192,2048]{1,0:T(8,128)(2,1)} %get-tuple-element.31), channel_id=1, source_target_pairs={{0,6},{1,7},{2,0},{3,1},{4,2},{5,3},{6,4},{7,5},{8,14},{9,15},{10,... | collective-permute-start | bytes 2359304 | tf_op jit(solution)/shard_map/ppermute | solution.py:378
  158.1 20.5 %collective-permute-start.5 = (bf16[192,2048]{1,0:T(8,128)(2,1)}, bf16[192,2048]{1,0:T(8,128)(2,1)}, u32[]{:S(2)}, u32[]{:S(2)}) collective-permute-start(bf16[192,2048]{1,0:T(8,128)(2,1)} %get-tuple-element.33), channel_id=1, source_target_pairs={{0,2},{1,3},{2,4},{3,5},{4,6},{5,7},{6,0},{7,1},{8,10},{9,11},{10,... | collective-permute-start | bytes 2359304 | tf_op jit(solution)/shard_map/ppermute | solution.py:375
  159.5 19.0 %copy-start = (bf16[384,2048]{1,0:T(8,128)(2,1)S(1)}, bf16[384,2048]{1,0:T(8,128)(2,1)}, u32[]{:S(2)}) copy-start(bf16[384,2048]{1,0:T(8,128)(2,1)} %get-tuple-element.21) | copy-start | bytes 4718596

commit v2 on v1

v2 whole, which is shorter than its diff:
```python
import functools

import jax
import jax.numpy as jnp
from jax import lax
from jax.experimental import pallas as pl
from jax.experimental.pallas import tpu as pltpu
from jax.sharding import PartitionSpec as P


MESH = pl.DeviceIdType.MESH
BF = jnp.bfloat16
F32 = jnp.float32
NT = (((1,), (1,)), ((), ()))
TN = (((0,), (0,)), ((), ()))

EARLY = 3

R_A, R_B, L_A, L_B, F_R, F_L, Q_OWN, Q_LA, Q_LB, Q_RA, Q_RB, Q_OA, Q_OB = range(13)


def gather_kernel(
    n, x, dy, wd, wg, wu, ug, uu,
    xg, dyg, dug, duu, dwd, s_own, s_la, s_lb0, s_lb, s_ra0, s_ra, s_rb, s_oa, s_ob, got_a, got_b,
    vwd, vwg, vwu, vdy, vug, vuu, vdug, vduu, vz, vp, vq, vdw,
    ss, rs, sx, rx, se, re, wsem, usem, dsem, osem, psem, qsem,
):
    rows, hid = x.shape
    half = rows // 2
    ff = wd.shape[0]
    me = lax.axis_index("tp")
    core = lax.rem(me, 2)
    right, left = lax.rem(me + 2, n), lax.rem(me + n - 2, n)
    opp = lax.rem(me + 4, n)
    mate = me + 1 - 2 * core

    def whole(d):
        return pl.ds(pl.multiple_of(d * rows, rows), rows)

    def part(d, h):
        return pl.ds(pl.multiple_of(d * rows + h * half, half), half)

    def at(slot):
        return pl.ds(slot * rows, rows)

    def send(src, dst, s_sem, r_sem, dev):
        return pltpu.make_async_remote_copy(
            src, dst, s_sem, r_sem, device_id={"tp": dev}, device_id_type=MESH
        )

    def remote(src, dst, k, i, dev):
        return send(src, dst, ss.at[k, i], rs.at[k, i], dev)

    gathers = ((dy, dyg), (x, xg))

    def send_own(k):
        src, dst = gathers[k]
        a, b = pl.ds(0, half), pl.ds(half, half)
        remote(src.at[a], dst.at[part(me, 0)], k, R_A, right).start()
        remote(src.at[b], dst.at[part(me, 1)], k, L_B, left).start()
        remote(src, dst.at[whole(me)], k, Q_OWN, mate).start()
        remote(src.at[b], dst.at[part(me, 1)], k, R_B, right).start()
        remote(src.at[a], dst.at[part(me, 0)], k, L_A, left).start()

    def piece(k, d, h, i, dev):
        dst = gathers[k][1]
        return remote(dst.at[part(d, h)], dst.at[part(d, h)], k, i, dev)

    def relay_first(k):
        piece(k, left, 0, R_A, right).wait_recv()
        piece(k, left, 0, F_R, right).start()
        piece(k, left, 0, Q_LA, mate).start()
        piece(k, right, 1, L_B, left).wait_recv()
        piece(k, right, 1, F_L, left).start()
        piece(k, right, 1, Q_RB, mate).start()

    def relay_second(k):
        piece(k, left, 1, R_B, right).wait_recv()
        piece(k, left, 1, Q_LB, mate).start()
        piece(k, right, 0, L_A, left).wait_recv()
        piece(k, right, 0, Q_RA, mate).start()

    def relay_third(k):
        piece(k, opp, 0, F_R, right).wait_recv()
        piece(k, opp, 0, Q_OA, mate).start()
        piece(k, opp, 1, F_L, left).wait_recv()
        piece(k, opp, 1, Q_OB, mate).start()

    def drain(k):
        src, dst = gathers[k]
        for i in (R_A, R_B, L_A, L_B, F_R, F_L, Q_LA, Q_LB, Q_RA, Q_RB, Q_OA, Q_OB):
            piece(k, me, 0, i, right).wait_send()
        remote(src, dst.at[whole(me)], k, Q_OWN, mate).wait_send()

    def wait_mate(k, *slots):
        for i in slots:
            piece(k, me, 0, i, mate).wait_recv()

    def own_from_mate(k):
        src, dst = gathers[k]
        remote(src, dst.at[whole(me)], k, Q_OWN, mate).wait_recv()

    barrier = pltpu.get_barrier_semaphore()
    for dev in (right, left, mate):
        pl.semaphore_signal(barrier, inc=1, device_id={"tp": dev}, device_id_type=MESH)
    pl.semaphore_wait(barrier, 3)
    send_own(0)

    chips = (me, left, right, opp)

    def device(j, slot):
        return chips[j] if slot == 1 else chips[j] + 1 - 2 * core

    def u_load(j, slot):
        return (
            pltpu.make_async_copy(ug.at[whole(device(j, slot))], vug.at[slot], usem.at[0, slot]),
            pltpu.make_async_copy(uu.at[whole(device(j, slot))], vuu.at[slot], usem.at[1, slot]),
        )

    def y_load(j, slot):
        i = 2 * (j % 2) + slot
        src = dy if j == 0 and slot == 1 else dyg.at[whole(device(j, slot))]
        return pltpu.make_async_copy(src, vdy.at[at(i)], dsem.at[i])

    def outs(j, slot):
        d = device(j, slot)
        return (
            pltpu.make_async_copy(vdug.at[slot], dug.at[whole(d)], osem.at[0, slot]),
            pltpu.make_async_copy(vduu.at[slot], duu.at[whole(d)], osem.at[1, slot]),
        )

    def p_out(j):
        if j == 0:
            return (pltpu.make_async_copy(vp.at[1], s_own, psem.at[0]),)
        dst = ((s_la, s_lb0, s_lb), (s_ra0, s_ra, s_rb), (s_oa, s_ob))[j - 1]
        copies, r = [], 0
        for i, o in enumerate(dst):
            copies.append(pltpu.make_async_copy(vp.at[1, pl.ds(r, o.shape[0])], o, psem.at[i]))
            r += o.shape[0]
        return copies

    def swap(j):
        return send(vp.at[0], vq.at[j % 2], sx.at[j], rx.at[j], mate)

    def start(copies):
        for c in copies:
            c.start()

    def wait(copies):
        for c in copies:
            c.wait()

    load_wd = pltpu.make_async_copy(wd, vwd, wsem.at[0])
    load_w = (pltpu.make_async_copy(wg, vwg, wsem.at[1]), pltpu.make_async_copy(wu, vwu, wsem.at[2]))
    own_x = (pltpu.make_async_copy(x, vdy.at[at(2)], dsem.at[2]), pltpu.make_async_copy(vdy.at[at(2)], xg.at[whole(me)], qsem.at[0]))
    y_load(0, 1).start()
    start(u_load(0, 1))
    load_wd.start()
    start(u_load(0, 0))
    start(load_w)
    own_x[0].start()

    gn, hn, nt = min(512, ff), min(1024, hid), min(512, hid)

    def gate(j, slot):
        y_load(j, slot).wait()
        wait(u_load(j, slot))
        if j > 0:
            wait(outs(j - 1, slot))

        @pl.loop(0, ff // gn)
        def _(i):
            cols = pl.ds(pl.multiple_of(i * gn, gn), gn)
            y = vdy[at(2 * (j % 2) + slot), :]
            g = lax.dot_general(y, vwd[cols, :], NT, preferred_element_type=F32)
            u = vug[slot, :, cols].astype(F32)
            v = vuu[slot, :, cols].astype(F32)
            s = jax.nn.sigmoid(u)
            a = u * s
            vz[at(slot), cols] = (a * v).astype(BF)
            vduu[slot, :, cols] = (g * a).astype(BF)
            vdug[slot, :, cols] = (g * v * s * (1.0 + u * (1.0 - s))).astype(BF)

        start(outs(j, slot))
        if j < 3:
            start(u_load(j + 1, slot))

    def partial(j, slot):
        @pl.loop(0, hid // hn)
        def _(i):
            cols = pl.ds(pl.multiple_of(i * hn, hn), hn)
            p = lax.dot_general(vdug[slot], vwg[cols, :], NT, preferred_element_type=F32)
            p += lax.dot_general(vduu[slot], vwu[cols, :], NT, preferred_element_type=F32)
            if slot == 1:
                p += vq[j % 2, :, cols].astype(F32)
            vp[slot, :, cols] = p.astype(BF)

    def down(j):
        base = 2 * rows * (j % 2)

        @pl.loop(0, ff // gn)
        def _(i):
            mine = pl.ds(pl.multiple_of(i * gn, gn), gn)
            zt = vz[:, mine]
            for k in range(0, hid, nt):
                y = vdy[pl.ds(base, 2 * rows), k : k + nt]
                q = lax.dot_general(zt, y, TN, preferred_element_type=F32)
                if j == 0:
                    vdw[mine, k : k + nt] = q
                else:
                    vdw[mine, k : k + nt] += q

    def chip(j, before_mate=None, before_down=None):
        gate(j, 1)
        if before_mate is not None:
            before_mate()
        gate(j, 0)
        if j == 0:
            wait(load_w)
        else:
            swap(j - 1).wait_send()
        partial(j, 0)
        swap(j).start()
        if before_down is not None:
            before_down()
        down(j)
        swap(j).wait_recv()
        if j > 0:
            wait(p_out(j - 1))
        partial(j, 1)
        start(p_out(j))

    def first_mate():
        own_from_mate(0)
        y_load(0, 0).start()
        own_x[0].wait()
        own_x[1].start()

    load_wd.wait()
    chip(0, before_mate=first_mate)
    own_x[1].wait()
    relay_first(0)
    send_own(1)
    relay_second(0)
    y_load(1, 1).start()
    wait_mate(0, Q_LA, Q_LB)
    y_load(1, 0).start()

    def fetch_right():
        y_load(2, 1).start()
        wait_mate(0, Q_RA, Q_RB)
        y_load(2, 0).start()

    chip(1, before_down=fetch_right)
    relay_third(0)

    def fetch_opp():
        y_load(3, 1).start()
        wait_mate(0, Q_OA, Q_OB)
        y_load(3, 0).start()

    chip(2, before_down=fetch_opp)
    relay_first(1)
    chip(3)
    dw_out = pltpu.make_async_copy(vdw, dwd, qsem.at[0])
    dw_out.start()
    near = (send(s_ra0, got_a, se.at[0], re.at[0], right), send(s_lb0, got_b, se.at[1], re.at[1], left))
    start(near)
    relay_second(1)
    relay_third(1)
    for slot in (0, 1):
        wait(outs(3, slot))
    wait(p_out(3))
    swap(3).wait_send()
    dw_out.wait()
    own_from_mate(1)
    wait_mate(1, Q_LA, Q_LB, Q_RA, Q_RB, Q_OA, Q_OB)
    wait(near)
    drain(0)
    drain(1)


def gather_and_local(n, x, dy, wd, wg, wu, ug, uu):
    rows, hid = x.shape
    tok, ff = ug.shape
    half = rows // 2
    early = half // EARLY
    any_ = pl.BlockSpec(memory_space=pl.ANY)
    sds = jax.ShapeDtypeStruct

    def r(k):
        return sds((k, hid), BF)

    out = [r(tok), r(tok), sds((tok, ff), BF), sds((tok, ff), BF), sds((ff, hid), F32), r(rows)]
    out += [r(half), r(early), r(half - early), r(early), r(half - early), r(half), r(half), r(half), r(early), r(early)]
    return pl.pallas_call(
        functools.partial(gather_kernel, n),
        out_shape=out,
        in_specs=[any_] * 7,
        out_specs=[any_] * len(out),
        scratch_shapes=[
            pltpu.VMEM(wd.shape, BF), pltpu.VMEM(wg.shape, BF), pltpu.VMEM(wu.shape, BF),
            pltpu.VMEM((4 * rows, hid), BF),
            pltpu.VMEM((2, rows, ff), BF), pltpu.VMEM((2, rows, ff), BF),
            pltpu.VMEM((2, rows, ff), BF), pltpu.VMEM((2, rows, ff), BF), pltpu.VMEM((2 * rows, ff), BF),
            pltpu.VMEM((2, rows, hid), BF),
            pltpu.VMEM((2, rows, hid), BF),
            pltpu.VMEM((ff, hid), F32),
            pltpu.SemaphoreType.DMA((2, 13)), pltpu.SemaphoreType.DMA((2, 13)),
            pltpu.SemaphoreType.DMA((4,)), pltpu.SemaphoreType.DMA((4,)),
            pltpu.SemaphoreType.DMA((2,)), pltpu.SemaphoreType.DMA((2,)),
            pltpu.SemaphoreType.DMA((3,)), pltpu.SemaphoreType.DMA((2, 2)), pltpu.SemaphoreType.DMA((4,)),
            pltpu.SemaphoreType.DMA((2, 2)), pltpu.SemaphoreType.DMA((3,)), pltpu.SemaphoreType.DMA((2,)),
        ],
        compiler_params=pltpu.CompilerParams(collective_id=0, has_side_effects=True, vmem_limit_bytes=62 * 2**20),
        cost_estimate=pl.CostEstimate(flops=8 * tok * hid * ff, bytes_accessed=100 * 2**20, transcendentals=tok * ff),
    )(x, dy, wd, wg, wu, ug, uu)


def tokens_kernel(kt, a, b, *refs):
    *thru, vb, sem = refs
    if len(thru) == 3:
        spare, o, spare_out = thru
        spare_out[...] = spare[...]
    else:
        (o,) = thru
    tok = a.shape[0]
    copies = [
        pltpu.make_async_copy(b.at[pl.ds(k, kt)], vb.at[pl.ds(k, kt)], sem.at[k // kt]) for k in range(0, tok, kt)
    ]

    @pl.when(pl.program_id(0) == 0)
    def _():
        for c in copies:
            c.start()
        for i, c in enumerate(copies):
            c.wait()
            ks = pl.ds(i * kt, kt)
            p = lax.dot_general(a[ks, :], vb[ks, :], TN, preferred_element_type=F32)
            if i == 0:
                o[...] = p
            else:
                o[...] += p

    @pl.when(pl.program_id(0) > 0)
    def _():
        o[...] = lax.dot_general(a[...], vb[...], TN, preferred_element_type=F32)


def over_tokens(a, b, spare=None, m_tile=256, kt=768):
    tok, m = a.shape
    k = b.shape[1]
    m_tile, kt = min(m_tile, m), min(kt, tok)
    steps = m // m_tile
    out_shape = [jax.ShapeDtypeStruct((m, k), F32)]
    in_specs = [pl.BlockSpec((tok, m_tile), lambda i: (0, i)), pl.BlockSpec(memory_space=pl.ANY)]
    out_specs = [pl.BlockSpec((m_tile, k), lambda i: (i, 0))]
    args = [a, b]
    if spare is not None:
        block = pl.BlockSpec((spare.shape[0] // steps, spare.shape[1]), lambda i: (i, 0))
        out_shape.append(jax.ShapeDtypeStruct(spare.shape, spare.dtype))
        in_specs.append(block)
        out_specs.append(block)
        args.append(spare)
    return pl.pallas_call(
        functools.partial(tokens_kernel, kt),
        grid=(steps,),
        out_shape=out_shape,
        in_specs=in_specs,
        out_specs=out_specs,
        scratch_shapes=[pltpu.VMEM((tok, k), BF), pltpu.SemaphoreType.DMA((tok // kt,))],
        compiler_params=pltpu.CompilerParams(vmem_limit_bytes=62 * 2**20),
        cost_estimate=pl.CostEstimate(
            flops=2 * tok * m * k, bytes_accessed=2 * tok * (m + k) + 4 * m * k, transcendentals=0
        ),
    )(*args)


def pair_kernel(a, b, c, d, ab, cd):
    ab[...] = (a[...].astype(F32) + b[...].astype(F32)).astype(BF)
    cd[...] = (c[...].astype(F32) + d[...].astype(F32)).astype(BF)


def pair_sum(a, b, c, d, steps=2):
    rows, hid = a.shape
    block = pl.BlockSpec((rows // steps, hid), lambda i: (i, 0))
    return pl.pallas_call(
        pair_kernel,
        grid=(steps,),
        out_shape=[jax.ShapeDtypeStruct(a.shape, BF)] * 2,
        in_specs=[block] * 4,
        out_specs=[block] * 2,
        compiler_params=pltpu.CompilerParams(vmem_limit_bytes=16 * 2**20),
        cost_estimate=pl.CostEstimate(flops=2 * rows * hid, bytes_accessed=12 * rows * hid, transcendentals=0),
    )(a, b, c, d)


def final_kernel(own, got_a, got_b, near_a, near_b, far_a, far_b, o):
    first = pl.program_id(0) == 0
    for i, (got, near, far) in enumerate(((got_a, near_a, far_a), (got_b, near_b, far_b))):
        direct = jnp.where(first, got[...], near[...]).astype(F32)
        o[i] = (own[i].astype(F32) + direct + far[...].astype(F32)).astype(BF)


def final_sum(own, got_a, got_b, near_a, near_b, far_a, far_b):
    rows, hid = own.shape
    half = rows // 2
    t = got_a.shape[0]
    both = pl.BlockSpec((2, t, hid), lambda i: (0, i, 0))
    one = pl.BlockSpec((t, hid), lambda i: (i, 0))
    got = pl.BlockSpec((t, hid), lambda i: (0, 0))
    near = pl.BlockSpec((t, hid), lambda i: (jnp.maximum(i - 1, 0), 0))
    return pl.pallas_call(
        final_kernel,
        grid=(half // t,),
        out_shape=jax.ShapeDtypeStruct((2, half, hid), BF),
        in_specs=[both, got, got, near, near, one, one],
        out_specs=both,
        compiler_params=pltpu.CompilerParams(vmem_limit_bytes=16 * 2**20),
        cost_estimate=pl.CostEstimate(flops=rows * hid * 3, bytes_accessed=8 * rows * hid, transcendentals=0),
    )(own.reshape(2, half, hid), got_a, got_b, near_a, near_b, far_a, far_b).reshape(rows, hid)


def solution(mesh):
    tok = P(("dp", "tp"), None)
    col = P(None, "tp")
    row = P("tp", None)
    act = P("dp", "tp")
    n = mesh.shape["tp"]
    to_right = [(i, (i + 2) % n) for i in range(n)]
    to_left = [(i, (i - 2) % n) for i in range(n)]

    def body(x, dy, wg, wu, wd, ug, uu):
        xg, _, dug, duu, dwd, s_own, s_la, _, s_lb, _, s_ra, s_rb, s_oa, s_ob, got_a, got_b = (
            gather_and_local(n, x, dy, wd, wg, wu, ug, uu)
        )

        def right(v):
            return lax.ppermute(v, "tp", to_right)

        def left(v):
            return lax.ppermute(v, "tp", to_left)

        from_right = left(s_oa)
        from_left = right(s_ob)
        direct_a = right(s_ra)
        direct_b = left(s_lb)
        (dwg,) = over_tokens(xg, dug)
        from_right, from_left, dwg = lax.optimization_barrier((from_right, from_left, dwg))
        next_l, next_r = pair_sum(s_la, from_right, s_rb, from_left)
        next_l, next_r, xg = lax.optimization_barrier((next_l, next_r, xg))
        relay_a = left(next_l)
        relay_b = right(next_r)
        dwu, dwd = over_tokens(xg, duu, spare=dwd)
        dx = final_sum(s_own, got_a, got_b, direct_a, direct_b, relay_a, relay_b)
        return dx, dwg, dwu, dwd

    return jax.shard_map(
        body, mesh=mesh, in_specs=(tok, tok, col, col, row, act, act), out_specs=(tok, act, act, tok), check_vma=False
    )
```

time: 192 us -> 178 us (0.927)
  local copies, waits for them, and re-layouts: 7.9 us -> 0.96 us
  waiting for transfers between devices: 13 us -> 7.52 us
  other arithmetic: 3.18 us -> 0 us
  Pallas kernels: 159 us -> 161 us
    ppermute x3, waiting for transfers between devices: 13 us -> 0.84 us  [right(): return lax.ppermute(v, 'tp', to_right)]
    unnamed x7 -> x10, local copies, waits for them, and re-layouts: 7.9 us -> 0.96 us
    ppermute x3, waiting for transfers between devices: 0.01 us -> 6.68 us  [left(): return lax.ppermute(v, 'tp', to_left)]
    pallas_call x3 -> x4, Pallas kernels: 42.2 us -> 47.9 us  [the longest x2 41.5 us: over_tokens(): pl.pallas_call(functools.partial(tokens_kernel, kt), grid=(steps,), out_s...]
    pallas_call x1, Pallas kernels: 117 us -> 113 us  [gather_and_local(): pl.pallas_call(functools.partial(gather_kernel, n), out_shape=out, in_spe...]
    convert_element_type x1 -> x0, other arithmetic: 3.18 us -> none  [add(): return functools.reduce(jnp.add, [t.astype(F32) for t in terms]).astype(BF)]
  transfers between devices with their start and end apart: 6 -> 6, of which waited for: 1 -> 2; matrix products, arithmetic and copies ran while one was open for 2% -> 0% of each run, Pallas kernels for 20% -> 25%
where the time goes in v2:
time: 178 us; the launch traced here: 176 us
  Pallas kernels  161 us (90%)
  waiting for transfers between devices  7.52 us (4%)
  starting transfers between devices  6.64 us (4%)
    pallas_call x1, Pallas kernels, gather_and_local(): pl.pallas_call(functools.partial(gather_kernel, n), out_shape=out, in_spe...  113 us
    pallas_call x2, Pallas kernels, over_tokens(): pl.pallas_call(functools.partial(tokens_kernel, kt), grid=(steps,), out_s...  41.5 us
    ppermute x3, waiting for transfers between devices, left(): return lax.ppermute(v, 'tp', to_left)  6.68 us
    ppermute x3, starting transfers between devices, left(): return lax.ppermute(v, 'tp', to_left)  4.93 us
    pallas_call x1, Pallas kernels, final_sum(): pl.pallas_call(final_kernel, grid=(half // t,), out_shape=jax.ShapeDtypeS...  4.01 us
  transfers between devices with their start and end apart: 6, of which 2 were waited for; matrix products, arithmetic and copies ran while one was open for 0% of the time, Pallas kernels for 25%

profile of v2, /device:TPU:81, one launch (start us, length us, event | category | flops | bytes accessed | tf_op | source)
XLA Modules:
  0.0 176.4 jit_solution(8537706984689285898)
XLA Ops:
  0.6 112.7 %shard_map.102 = (bf16[3072,2048]{1,0:T(8,128)(2,1)}, bf16[3072,2048]{1,0:T(8,128)(2,1)}, bf16[3072,1024]{1,0:T(8,128)(2,1)}, bf16[3072,1024]{1,0:T(8,128)(2,1)}...) custom-call(bf16[384,2048]{1,0:T(8,128)(2,1)} %x.1, ...), custom_call_target="tpu_custom_call" | custom-call | flops 51539607552 | bytes 104857600 | tf_op jit(solution)/shard_map/pallas_call | solution.py:296
  113.3 0.8 collective-permute-start
  114.1 1.9 %collective-permute-start.1 = (bf16[128,2048]{1,0:T(8,128)(2,1)}, bf16[128,2048]{1,0:T(8,128)(2,1)}, u32[]{:S(2)}, u32[]{:S(2)}) collective-permute-start(bf16[128,2048]{1,0:T(8,128)(2,1)} %get-tuple-element.31), channel_id=1, source_target_pairs={{0,6},{1,7},{2,0},{3,1},{4,2},{5,3},{6,4},{7,5},{8,14},{9,15},{10,... | collective-permute-start | bytes 1572872 | tf_op jit(solution)/shard_map/ppermute | solution.py:442
  116.1 0.6 collective-permute-start.2
  116.7 0.9 collective-permute-start.3
  117.5 0.0 copy-start.1
  117.5 0.0 copy-start.2
  117.5 19.0 %shard_map.103 = f32[2048,1024]{1,0:T(8,128)} custom-call(bf16[3072,2048]{1,0:T(8,128)(2,1)} %get-tuple-element.45.a, bf16[3072,1024]{1,0:T(8,128)(2,1)} %get-tuple-element.36.b), custom_call_target="tpu_custom_call" | custom-call | flops 12884901888 | bytes 27262976 | tf_op jit(solution)/shard_map/pallas_call | solution.py:365
  136.5 6.7 %collective-permute-done.2.b = bf16[192,2048]{1,0:T(8,128)(2,1)} collective-permute-done((bf16[192,2048]{1,0:T(8,128)(2,1)}, bf16[192,2048]{1,0:T(8,128)(2,1)}, u32[]{:S(2)}, u32[]{:S(2)}) %collective-permute-start.2) | collective-permute-done | bytes 786464 | tf_op jit(solution)/shard_map/ppermute | solution.py:442
  143.2 0.8 collective-permute-done.3.d
  144.0 0.0 copy-done.1
  144.0 0.0 copy-done.2
  144.0 2.4 %shard_map.104 = (bf16[192,2048]{1,0:T(8,128)(2,1)}, bf16[192,2048]{1,0:T(8,128)(2,1)}) custom-call(bf16[192,2048]{1,0:T(8,128)(2,1)S(1)} %copy-done.1, bf16[192,2048]{1,0:T(8,128)(2,1)} %collective-permute-done.2.b, bf16[192,2048]{1,0:T(8,128)(2,1)S(1)} %copy-done.2, bf16[192,2048]{1,0:T(8,128)(2,1)} %collective-permute-done.3.d), custom_call_target="tpu_custom_call" | custom-call | flops 786432 | bytes 4718592 | tf_op jit(solution)/shard_map/pallas_call | solution.py:387
  146.4 2.4 %collective-permute-start.4 = (bf16[192,2048]{1,0:T(8,128)(2,1)}, bf16[192,2048]{1,0:T(8,128)(2,1)}, u32[]{:S(2)}, u32[]{:S(2)}) collective-permute-start(bf16[192,2048]{1,0:T(8,128)(2,1)} %get-tuple-element.42), channel_id=1, source_target_pairs={{0,6},{1,7},{2,0},{3,1},{4,2},{5,3},{6,4},{7,5},{8,14},{9,15},{10,... | collective-permute-start | bytes 2359304 | tf_op jit(solution)/shard_map/ppermute | solution.py:442
  148.8 0.0 collective-permute-start.5
  148.8 0.0 copy-start
  148.8 0.0 copy-start.3
  148.8 22.5 %shard_map.106 = (f32[2048,1024]{1,0:T(8,128)}, f32[1024,2048]{1,0:T(8,128)}) custom-call(bf16[3072,2048]{1,0:T(8,128)(2,1)} %get-tuple-element.45.a, bf16[3072,1024]{1,0:T(8,128)(2,1)} %get-tuple-element.46.b, f32[1024,2048]{1,0:T(8,128)} %get-tuple-element.47.refs_0_), custom_call_target="tpu_custom_call" | custom-call | flops 12884901888 | bytes 27262976 | tf_op jit(solution)/shard_map/pallas_call | solution.py:365
  171.4 0.0 collective-permute-done.near_a
  171.4 0.0 collective-permute-done.1.near_b
  171.4 0.0 collective-permute-done.4.far_a
  171.4 0.0 collective-permute-done.5.far_b
  171.4 0.0 copy-done
  171.4 0.0 copy-done.3
  171.4 0.0 copy-start.4
  171.4 0.9 copy-done.4
  172.4 4.0 %shard_map.105 = bf16[2,192,2048]{2,1,0:T(8,128)(2,1)} custom-call(bf16[2,192,2048]{2,1,0:T(8,128)(2,1)S(1)} %bitcast.2, bf16[64,2048]{1,0:T(8,128)(2,1)S(1)} %copy-done.3, bf16[64,2048]{1,0:T(8,128)(2,1)S(1)} %copy-done.4, bf16[128,2048]{1,0:T(8,128)(2,1)} %collective-permute-done.near_a, bf16[128,2048]{1,0:T(8,128)(2,1)} %collective-permute-done.1.near_b, ...), custom_call_target="tpu_custom_call" | custom-call | flops 2359296 | bytes 6291456 | tf_op jit(solution)/shard_map/pallas_call | solution.py:413
Async XLA Ops:
  113.3 58.1 %collective-permute-start = (bf16[128,2048]{1,0:T(8,128)(2,1)}, bf16[128,2048]{1,0:T(8,128)(2,1)}, u32[]{:S(2)}, u32[]{:S(2)}) collective-permute-start(bf16[128,2048]{1,0:T(8,128)(2,1)} %get-tuple-element.30), channel_id=1, source_target_pairs={{0,2},{1,3},{2,4},{3,5},{4,6},{5,7},{6,0},{7,1},{8,10},{9,11},{10,... | collective-permute-start | bytes 1572872 | tf_op jit(solution)/shard_map/ppermute | solution.py:439
  114.1 57.2 %collective-permute-start.1 = (bf16[128,2048]{1,0:T(8,128)(2,1)}, bf16[128,2048]{1,0:T(8,128)(2,1)}, u32[]{:S(2)}, u32[]{:S(2)}) collective-permute-start(bf16[128,2048]{1,0:T(8,128)(2,1)} %get-tuple-element.31), channel_id=1, source_target_pairs={{0,6},{1,7},{2,0},{3,1},{4,2},{5,3},{6,4},{7,5},{8,14},{9,15},{10,... | collective-permute-start | bytes 1572872 | tf_op jit(solution)/shard_map/ppermute | solution.py:442
  116.1 27.1 %collective-permute-start.2 = (bf16[192,2048]{1,0:T(8,128)(2,1)}, bf16[192,2048]{1,0:T(8,128)(2,1)}, u32[]{:S(2)}, u32[]{:S(2)}) collective-permute-start(bf16[192,2048]{1,0:T(8,128)(2,1)} %get-tuple-element.33), channel_id=1, source_target_pairs={{0,6},{1,7},{2,0},{3,1},{4,2},{5,3},{6,4},{7,5},{8,14},{9,15},{10,... | collective-permute-start | bytes 2359304 | tf_op jit(solution)/shard_map/ppermute | solution.py:442
  116.7 27.4 %collective-permute-start.3 = (bf16[192,2048]{1,0:T(8,128)(2,1)}, bf16[192,2048]{1,0:T(8,128)(2,1)}, u32[]{:S(2)}, u32[]{:S(2)}) collective-permute-start(bf16[192,2048]{1,0:T(8,128)(2,1)} %get-tuple-element.34), channel_id=1, source_target_pairs={{0,2},{1,3},{2,4},{3,5},{4,6},{5,7},{6,0},{7,1},{8,10},{9,11},{10,... | collective-permute-start | bytes 2359304 | tf_op jit(solution)/shard_map/ppermute | solution.py:439
  117.5 26.5 %copy-start.1 = (bf16[192,2048]{1,0:T(8,128)(2,1)S(1)}, bf16[192,2048]{1,0:T(8,128)(2,1)}, u32[]{:S(2)}) copy-start(bf16[192,2048]{1,0:T(8,128)(2,1)} %get-tuple-element.32.a) | copy-start | bytes 2359300
  117.5 26.5 %copy-start.2 = (bf16[192,2048]{1,0:T(8,128)(2,1)S(1)}, bf16[192,2048]{1,0:T(8,128)(2,1)}, u32[]{:S(2)}) copy-start(bf16[192,2048]{1,0:T(8,128)(2,1)} %get-tuple-element.38.c) | copy-start | bytes 2359300
  146.4 25.0 %collective-permute-start.4 = (bf16[192,2048]{1,0:T(8,128)(2,1)}, bf16[192,2048]{1,0:T(8,128)(2,1)}, u32[]{:S(2)}, u32[]{:S(2)}) collective-permute-start(bf16[192,2048]{1,0:T(8,128)(2,1)} %get-tuple-element.42), channel_id=1, source_target_pairs={{0,6},{1,7},{2,0},{3,1},{4,2},{5,3},{6,4},{7,5},{8,14},{9,15},{10,... | collective-permute-start | bytes 2359304 | tf_op jit(solution)/shard_map/ppermute | solution.py:442
  148.8 22.6 %collective-permute-start.5 = (bf16[192,2048]{1,0:T(8,128)(2,1)}, bf16[192,2048]{1,0:T(8,128)(2,1)}, u32[]{:S(2)}, u32[]{:S(2)}) collective-permute-start(bf16[192,2048]{1,0:T(8,128)(2,1)} %get-tuple-element.43), channel_id=1, source_target_pairs={{0,2},{1,3},{2,4},{3,5},{4,6},{5,7},{6,0},{7,1},{8,10},{9,11},{10,... | collective-permute-start | bytes 2359304 | tf_op jit(solution)/shard_map/ppermute | solution.py:439
  148.8 22.6 %copy-start = (bf16[384,2048]{1,0:T(8,128)(2,1)S(1)}, bf16[384,2048]{1,0:T(8,128)(2,1)}, u32[]{:S(2)}) copy-start(bf16[384,2048]{1,0:T(8,128)(2,1)} %get-tuple-element.27) | copy-start | bytes 4718596
  148.8 22.6 %copy-start.3 = (bf16[64,2048]{1,0:T(8,128)(2,1)S(1)}, bf16[64,2048]{1,0:T(8,128)(2,1)}, u32[]{:S(2)}) copy-start(bf16[64,2048]{1,0:T(8,128)(2,1)} %get-tuple-element.28.got_a) | copy-start | bytes 786436
  171.4 1.0 copy-start.4

commit v3 on v2

--- a/solution.py
+++ b/solution.py
@@ -17,13 +17,14 @@
 EARLY = 3
 
 R_A, R_B, L_A, L_B, F_R, F_L, Q_OWN, Q_LA, Q_LB, Q_RA, Q_RB, Q_OA, Q_OB = range(13)
+LEFT, RIGHT, OPP, OWN = range(4)
 
 
 def gather_kernel(
     n, x, dy, wd, wg, wu, ug, uu,
-    xg, dyg, dug, duu, dwd, s_own, s_la, s_lb0, s_lb, s_ra0, s_ra, s_rb, s_oa, s_ob, got_a, got_b,
-    vwd, vwg, vwu, vdy, vug, vuu, vdug, vduu, vz, vp, vq, vdw,
-    ss, rs, sx, rx, se, re, wsem, usem, dsem, osem, psem, qsem,
+    xg, dyg, dug, duu, dwd, part_g, part_u, s_own, s_la, s_lb0, s_lb, s_ra0, s_ra, s_rb, s_oa, s_ob, got_a, got_b,
+    vwd, vwg, vwu, vdy, vug, vuu, vdug, vduu, vz, vp, vq, vdw, vt,
+    ss, rs, sx, rx, se, re, wsem, usem, dsem, osem, psem, qsem, tsem,
 ):
     rows, hid = x.shape
     half = rows // 2
@@ -37,8 +38,11 @@
     def whole(d):
         return pl.ds(pl.multiple_of(d * rows, rows), rows)
 
-    def part(d, h):
-        return pl.ds(pl.multiple_of(d * rows + h * half, half), half)
+    def pos(rel, c):
+        return pl.ds(pl.multiple_of((2 * rel + c) * rows, rows), rows)
+
+    def part(rel, h):
+        return pl.ds(pl.multiple_of((2 * rel + core) * rows + h * half, half), half)
 
     def at(slot):
         return pl.ds(slot * rows, rows)
@@ -56,60 +60,65 @@
     def send_own(k):
         src, dst = gathers[k]
         a, b = pl.ds(0, half), pl.ds(half, half)
-        remote(src.at[a], dst.at[part(me, 0)], k, R_A, right).start()
-        remote(src.at[b], dst.at[part(me, 1)], k, L_B, left).start()
-        remote(src, dst.at[whole(me)], k, Q_OWN, mate).start()
-        remote(src.at[b], dst.at[part(me, 1)], k, R_B, right).start()
-        remote(src.at[a], dst.at[part(me, 0)], k, L_A, left).start()
-
-    def piece(k, d, h, i, dev):
+        remote(src.at[a], dst.at[part(LEFT, 0)], k, R_A, right).start()
+        remote(src.at[b], dst.at[part(RIGHT, 1)], k, L_B, left).start()
+        remote(src.at[b], dst.at[part(LEFT, 1)], k, R_B, right).start()
+        remote(src.at[a], dst.at[part(RIGHT, 0)], k, L_A, left).start()
+
+    def own_to_mate(k):
+        src, dst = gathers[k]
+        return remote(src, dst.at[pos(OWN, core)], k, Q_OWN, mate)
+
+    def piece(k, rel, h, i, dev, to=None):
         dst = gathers[k][1]
-        return remote(dst.at[part(d, h)], dst.at[part(d, h)], k, i, dev)
+        return remote(dst.at[part(rel, h)], dst.at[part(rel if to is None else to, h)], k, i, dev)
 
     def relay_first(k):
-        piece(k, left, 0, R_A, right).wait_recv()
-        piece(k, left, 0, F_R, right).start()
-        piece(k, left, 0, Q_LA, mate).start()
-        piece(k, right, 1, L_B, left).wait_recv()
-        piece(k, right, 1, F_L, left).start()
-        piece(k, right, 1, Q_RB, mate).start()
+        piece(k, LEFT, 0, R_A, right).wait_recv()
+        piece(k, LEFT, 0, F_R, right, OPP).start()
+        piece(k, LEFT, 0, Q_LA, mate).start()
+        piece(k, RIGHT, 1, L_B, left).wait_recv()
+        piece(k, RIGHT, 1, F_L, left, OPP).start()
+        piece(k, RIGHT, 1, Q_RB, mate).start()
 
     def relay_second(k):
-        piece(k, left, 1, R_B, right).wait_recv()
-        piece(k, left, 1, Q_LB, mate).start()
-        piece(k, right, 0, L_A, left).wait_recv()
-        piece(k, right, 0, Q_RA, mate).start()
+        piece(k, LEFT, 1, R_B, right).wait_recv()
+        piece(k, LEFT, 1, Q_LB, mate).start()
+        piece(k, RIGHT, 0, L_A, left).wait_recv()
+        piece(k, RIGHT, 0, Q_RA, mate).start()
 
     def relay_third(k):
-        piece(k, opp, 0, F_R, right).wait_recv()
-        piece(k, opp, 0, Q_OA, mate).start()
-        piece(k, opp, 1, F_L, left).wait_recv()
-        piece(k, opp, 1, Q_OB, mate).start()
+        piece(k, OPP, 0, F_R, right).wait_recv()
+        piece(k, OPP, 0, Q_OA, mate).start()
+        piece(k, OPP, 1, F_L, left).wait_recv()
+        piece(k, OPP, 1, Q_OB, mate).start()
 
     def drain(k):
-        src, dst = gathers[k]
         for i in (R_A, R_B, L_A, L_B, F_R, F_L, Q_LA, Q_LB, Q_RA, Q_RB, Q_OA, Q_OB):
-            piece(k, me, 0, i, right).wait_send()
-        remote(src, dst.at[whole(me)], k, Q_OWN, mate).wait_send()
+            piece(k, OWN, 0, i, right).wait_send()
+        own_to_mate(k).wait_send()
 
     def wait_mate(k, *slots):
         for i in slots:
-            piece(k, me, 0, i, mate).wait_recv()
-
-    def own_from_mate(k):
-        src, dst = gathers[k]
-        remote(src, dst.at[whole(me)], k, Q_OWN, mate).wait_recv()
+            piece(k, OWN, 0, i, mate).wait_recv()
 
     barrier = pltpu.get_barrier_semaphore()
     for dev in (right, left, mate):
         pl.semaphore_signal(barrier, inc=1, device_id={"tp": dev}, device_id_type=MESH)
     pl.semaphore_wait(barrier, 3)
+    own_to_mate(0).start()
     send_own(0)
+    own_to_mate(1).start()
 
     chips = (me, left, right, opp)
 
     def device(j, slot):
         return chips[j] if slot == 1 else chips[j] + 1 - 2 * core
+
+    places = (OWN, LEFT, RIGHT, OPP)
+
+    def place(j, slot):
+        return pos(places[j], core if slot == 1 else 1 - core)
 
     def u_load(j, slot):
         return (
@@ -119,14 +128,13 @@
 
     def y_load(j, slot):
         i = 2 * (j % 2) + slot
-        src = dy if j == 0 and slot == 1 else dyg.at[whole(device(j, slot))]
+        src = dy if j == 0 and slot == 1 else dyg.at[place(j, slot)]
         return pltpu.make_async_copy(src, vdy.at[at(i)], dsem.at[i])
 
     def outs(j, slot):
-        d = device(j, slot)
         return (
-            pltpu.make_async_copy(vdug.at[slot], dug.at[whole(d)], osem.at[0, slot]),
-            pltpu.make_async_copy(vduu.at[slot], duu.at[whole(d)], osem.at[1, slot]),
+            pltpu.make_async_copy(vdug.at[slot], dug.at[place(j, slot)], osem.at[0, slot]),
+            pltpu.make_async_copy(vduu.at[slot], duu.at[place(j, slot)], osem.at[1, slot]),
         )
 
     def p_out(j):
@@ -152,13 +160,14 @@
 
     load_wd = pltpu.make_async_copy(wd, vwd, wsem.at[0])
     load_w = (pltpu.make_async_copy(wg, vwg, wsem.at[1]), pltpu.make_async_copy(wu, vwu, wsem.at[2]))
-    own_x = (pltpu.make_async_copy(x, vdy.at[at(2)], dsem.at[2]), pltpu.make_async_copy(vdy.at[at(2)], xg.at[whole(me)], qsem.at[0]))
+    own_x = pltpu.make_async_copy(x, vdy.at[at(3)], dsem.at[3])
+    mate_x = pltpu.make_async_copy(xg.at[pos(OWN, 1 - core)], vdy.at[at(2)], dsem.at[2])
     y_load(0, 1).start()
     start(u_load(0, 1))
     load_wd.start()
     start(u_load(0, 0))
     start(load_w)
-    own_x[0].start()
+    own_x.start()
 
     gn, hn, nt = min(512, ff), min(1024, hid), min(512, hid)
 
@@ -231,16 +240,43 @@
         start(p_out(j))
 
     def first_mate():
-        own_from_mate(0)
+        own_to_mate(0).wait_recv()
         y_load(0, 0).start()
-        own_x[0].wait()
-        own_x[1].start()
+
+    def first_down():
+        own_to_mate(1).wait_recv()
+        mate_x.start()
+
+    def own_tokens():
+        mt = vt.shape[1]
+        for src, out in ((vdug, part_g), (vduu, part_u)):
+
+            def leave(r, i):
+                return pltpu.make_async_copy(vt.at[i], out.at[pl.ds(pl.multiple_of(r, mt), mt)], tsem.at[i])
+
+            @pl.loop(0, hid // (2 * mt))
+            def _(t):
+                for i in (0, 1):
+                    r = (2 * t + i) * mt
+
+                    @pl.when(t > 0)
+                    def _():
+                        leave(r, i).wait()
+
+                    xt = vdy[pl.ds(2 * rows, 2 * rows), pl.ds(pl.multiple_of(r, mt), mt)]
+                    vt[i] = lax.dot_general(xt, src[...].reshape(2 * rows, ff), TN, preferred_element_type=F32)
+                    leave(r, i).start()
+
+            for i in (0, 1):
+                leave(i * mt, i).wait()
 
     load_wd.wait()
-    chip(0, before_mate=first_mate)
-    own_x[1].wait()
+    chip(0, before_mate=first_mate, before_down=first_down)
     relay_first(0)
     send_own(1)
+    own_x.wait()
+    mate_x.wait()
+    own_tokens()
     relay_second(0)
     y_load(1, 1).start()
     wait_mate(0, Q_LA, Q_LB)
@@ -273,7 +309,6 @@
     wait(p_out(3))
     swap(3).wait_send()
     dw_out.wait()
-    own_from_mate(1)
     wait_mate(1, Q_LA, Q_LB, Q_RA, Q_RB, Q_OA, Q_OB)
     wait(near)
     drain(0)
@@ -291,7 +326,8 @@
     def r(k):
         return sds((k, hid), BF)
 
-    out = [r(tok), r(tok), sds((tok, ff), BF), sds((tok, ff), BF), sds((ff, hid), F32), r(rows)]
+    out = [r(tok), r(tok), sds((tok, ff), BF), sds((tok, ff), BF), sds((ff, hid), F32)]
+    out += [sds((hid, ff), F32), sds((hid, ff), F32), r(rows)]
     out += [r(half), r(early), r(half - early), r(early), r(half - early), r(half), r(half), r(half), r(early), r(early)]
     return pl.pallas_call(
         functools.partial(gather_kernel, n),
@@ -306,56 +342,39 @@
             pltpu.VMEM((2, rows, hid), BF),
             pltpu.VMEM((2, rows, hid), BF),
             pltpu.VMEM((ff, hid), F32),
+            pltpu.VMEM((2, min(256, hid), ff), F32),
             pltpu.SemaphoreType.DMA((2, 13)), pltpu.SemaphoreType.DMA((2, 13)),
             pltpu.SemaphoreType.DMA((4,)), pltpu.SemaphoreType.DMA((4,)),
             pltpu.SemaphoreType.DMA((2,)), pltpu.SemaphoreType.DMA((2,)),
             pltpu.SemaphoreType.DMA((3,)), pltpu.SemaphoreType.DMA((2, 2)), pltpu.SemaphoreType.DMA((4,)),
-            pltpu.SemaphoreType.DMA((2, 2)), pltpu.SemaphoreType.DMA((3,)), pltpu.SemaphoreType.DMA((2,)),
+            pltpu.SemaphoreType.DMA((2, 2)), pltpu.SemaphoreType.DMA((3,)), pltpu.SemaphoreType.DMA((2,)), pltpu.SemaphoreType.DMA((2,)),
         ],
         compiler_params=pltpu.CompilerParams(collective_id=0, has_side_effects=True, vmem_limit_bytes=62 * 2**20),
         cost_estimate=pl.CostEstimate(flops=8 * tok * hid * ff, bytes_accessed=100 * 2**20, transcendentals=tok * ff),
     )(x, dy, wd, wg, wu, ug, uu)
 
 
-def tokens_kernel(kt, a, b, *refs):
-    *thru, vb, sem = refs
-    if len(thru) == 3:
-        spare, o, spare_out = thru
+def tokens_kernel(a, b, init, *refs):
+    if len(refs) == 3:
+        spare, o, spare_out = refs
         spare_out[...] = spare[...]
     else:
-        (o,) = thru
-    tok = a.shape[0]
-    copies = [
-        pltpu.make_async_copy(b.at[pl.ds(k, kt)], vb.at[pl.ds(k, kt)], sem.at[k // kt]) for k in range(0, tok, kt)
-    ]
-
-    @pl.when(pl.program_id(0) == 0)
-    def _():
-        for c in copies:
-            c.start()
-        for i, c in enumerate(copies):
-            c.wait()
-            ks = pl.ds(i * kt, kt)
-            p = lax.dot_general(a[ks, :], vb[ks, :], TN, preferred_element_type=F32)
-            if i == 0:
-                o[...] = p
-            else:
-                o[...] += p
-
-    @pl.when(pl.program_id(0) > 0)
-    def _():
-        o[...] = lax.dot_general(a[...], vb[...], TN, preferred_element_type=F32)
-
-
-def over_tokens(a, b, spare=None, m_tile=256, kt=768):
-    tok, m = a.shape
+        (o,) = refs
+    o[...] = init[...] + lax.dot_general(a[...], b[...], TN, preferred_element_type=F32)
+
+
+def over_tokens(a, b, init, spare=None, m_tile=512):
+    m = a.shape[1]
+    tok = a.shape[0] // 4 * 3
     k = b.shape[1]
-    m_tile, kt = min(m_tile, m), min(kt, tok)
+    m_tile = min(m_tile, m)
     steps = m // m_tile
+    tile = pl.BlockSpec((m_tile, k), lambda i: (i, 0))
+    whole = pl.BlockSpec((tok, k), lambda i: (0, 0), pipeline_mode=pl.Buffered(1))
     out_shape = [jax.ShapeDtypeStruct((m, k), F32)]
-    in_specs = [pl.BlockSpec((tok, m_tile), lambda i: (0, i)), pl.BlockSpec(memory_space=pl.ANY)]
-    out_specs = [pl.BlockSpec((m_tile, k), lambda i: (i, 0))]
-    args = [a, b]
+    in_specs = [pl.BlockSpec((tok, m_tile), lambda i: (0, i)), whole, tile]
+    out_specs = [tile]
+    args = [a, b, init]
     if spare is not None:
         block = pl.BlockSpec((spare.shape[0] // steps, spare.shape[1]), lambda i: (i, 0))
         out_shape.append(jax.ShapeDtypeStruct(spare.shape, spare.dtype))
@@ -363,15 +382,14 @@
         out_specs.append(block)
         args.append(spare)
     return pl.pallas_call(
-        functools.partial(tokens_kernel, kt),
+        tokens_kernel,
         grid=(steps,),
         out_shape=out_shape,
         in_specs=in_specs,
         out_specs=out_specs,
-        scratch_shapes=[pltpu.VMEM((tok, k), BF), pltpu.SemaphoreType.DMA((tok // kt,))],
-        compiler_params=pltpu.CompilerParams(vmem_limit_bytes=62 * 2**20),
+        compiler_params=pltpu.CompilerParams(vmem_limit_bytes=36 * 2**20),
         cost_estimate=pl.CostEstimate(
-            flops=2 * tok * m * k, bytes_accessed=2 * tok * (m + k) + 4 * m * k, transcendentals=0
+            flops=2 * tok * m * k, bytes_accessed=2 * tok * (m + k) + 8 * m * k, transcendentals=0
         ),
     )(*args)
 
@@ -431,7 +449,7 @@
     to_left = [(i, (i - 2) % n) for i in range(n)]
 
     def body(x, dy, wg, wu, wd, ug, uu):
-        xg, _, dug, duu, dwd, s_own, s_la, _, s_lb, _, s_ra, s_rb, s_oa, s_ob, got_a, got_b = (
+        xg, _, dug, duu, dwd, part_g, part_u, s_own, s_la, _, s_lb, _, s_ra, s_rb, s_oa, s_ob, got_a, got_b = (
             gather_and_local(n, x, dy, wd, wg, wu, ug, uu)
         )
 
@@ -445,13 +463,13 @@
         from_left = right(s_ob)
         direct_a = right(s_ra)
         direct_b = left(s_lb)
-        (dwg,) = over_tokens(xg, dug)
+        (dwg,) = over_tokens(xg, dug, part_g)
         from_right, from_left, dwg = lax.optimization_barrier((from_right, from_left, dwg))
         next_l, next_r = pair_sum(s_la, from_right, s_rb, from_left)
         next_l, next_r, xg = lax.optimization_barrier((next_l, next_r, xg))
         relay_a = left(next_l)
         relay_b = right(next_r)
-        dwu, dwd = over_tokens(xg, duu, spare=dwd)
+        dwu, dwd = over_tokens(xg, duu, part_u, spare=dwd)
         dx = final_sum(s_own, got_a, got_b, direct_a, direct_b, relay_a, relay_b)
         return dx, dwg, dwu, dwd
 

time: 178 us -> 171 us (0.961)
  Pallas kernels: 161 us -> 146 us
  local copies, waits for them, and re-layouts: 0.96 us -> 9.57 us
    pallas_call x2, Pallas kernels: 41.5 us -> 30.4 us  [over_tokens(): pl.pallas_call(tokens_kernel, grid=(steps,), out_shape=out_shape, in_spec...]
    unnamed x10 -> x18, local copies, waits for them, and re-layouts: 0.96 us -> 9.57 us
    pallas_call x1, Pallas kernels: 2.39 us -> 0.38 us  [pair_sum(): pl.pallas_call(pair_kernel, grid=(steps,), out_shape=[jax.ShapeDtypeStruc...]
    pallas_call x1, Pallas kernels: 4.01 us -> 2.12 us  [final_sum(): pl.pallas_call(final_kernel, grid=(half // t,), out_shape=jax.ShapeDtypeS...]
  transfers between devices with their start and end apart: 6 -> 6, of which waited for: 2 -> 2; matrix products, arithmetic and copies ran while one was open for 0% -> 0% of each run, Pallas kernels for 25% -> 18%
where the time goes in v3:
time: 171 us; the launch traced here: 169 us
  Pallas kernels  146 us (85%)
  local copies, waits for them, and re-layouts  9.57 us (6%)
  starting transfers between devices  6.75 us (4%)
  waiting for transfers between devices  6.53 us (4%)
    pallas_call x1, Pallas kernels, gather_and_local(): pl.pallas_call(functools.partial(gather_kernel, n), out_shape=out, in_spe...  113 us
    pallas_call x2, Pallas kernels, over_tokens(): pl.pallas_call(tokens_kernel, grid=(steps,), out_shape=out_shape, in_spec...  30.4 us
    unnamed x18, local copies, waits for them, and re-layouts  9.57 us
    ppermute x3, waiting for transfers between devices, left(): return lax.ppermute(v, 'tp', to_left)  5.69 us
    ppermute x3, starting transfers between devices, left(): return lax.ppermute(v, 'tp', to_left)  5.03 us
  transfers between devices with their start and end apart: 6, of which 2 were waited for; matrix products, arithmetic and copies ran while one was open for 0% of the time, Pallas kernels for 18%

profile of v3, /device:TPU:81, one launch (start us, length us, event | category | flops | bytes accessed | tf_op | source)
XLA Modules:
  0.0 169.2 jit_solution(12007911619879743037)
XLA Ops:
  0.6 112.7 %shard_map.102 = (bf16[3072,2048]{1,0:T(8,128)(2,1)}, bf16[3072,2048]{1,0:T(8,128)(2,1)}, bf16[3072,1024]{1,0:T(8,128)(2,1)}, bf16[3072,1024]{1,0:T(8,128)(2,1)}...) custom-call(bf16[384,2048]{1,0:T(8,128)(2,1)} %x.1, ...), custom_call_target="tpu_custom_call" | custom-call | flops 51539607552 | bytes 104857600 | tf_op jit(solution)/shard_map/pallas_call | solution.py:332
  113.3 0.8 collective-permute-start
  114.2 1.9 %collective-permute-start.1 = (bf16[128,2048]{1,0:T(8,128)(2,1)}, bf16[128,2048]{1,0:T(8,128)(2,1)S(1)}, u32[]{:S(2)}, u32[]{:S(2)}) collective-permute-start(bf16[128,2048]{1,0:T(8,128)(2,1)} %get-tuple-element.33), channel_id=1, source_target_pairs={{0,6},{1,7},{2,0},{3,1},{4,2},{5,3},{6,4},{7,5},{8,14},{9,15},{10,... | collective-permute-start | bytes 1572872 | tf_op jit(solution)/shard_map/ppermute | solution.py:460
  116.1 0.6 collective-permute-start.2
  116.7 0.9 collective-permute-start.3
  117.6 0.0 copy-start.6
  117.6 3.4 %copy-done.6 = f32[2048,1024]{1,0:T(8,128)S(1)} copy-done((f32[2048,1024]{1,0:T(8,128)S(1)}, f32[2048,1024]{1,0:T(8,128)}, u32[]{:S(2)}) %copy-start.6) | copy-done | bytes 8388632
  120.9 0.0 copy-start.8
  120.9 2.8 %copy-done.8 = bf16[3072,1024]{1,0:T(8,128)(2,1)S(1)} copy-done((bf16[3072,1024]{1,0:T(8,128)(2,1)S(1)}, bf16[3072,1024]{1,0:T(8,128)(2,1)}, u32[]{:S(2)}) %copy-start.8) | copy-done | bytes 6291480
  123.7 0.0 copy-start.1
  123.7 0.0 copy-start.2
  123.7 0.0 copy-start.7
  123.7 13.7 %shard_map.103 = f32[2048,1024]{1,0:T(8,128)} custom-call(bf16[3072,2048]{1,0:T(8,128)(2,1)} %get-tuple-element.48.a, bf16[3072,1024]{1,0:T(8,128)(2,1)S(1)} %copy-done.8, f32[2048,1024]{1,0:T(8,128)S(1)} %copy-done.6), custom_call_target="tpu_custom_call" | custom-call | flops 9663676416 | bytes 30932992 | tf_op jit(solution)/shard_map/pallas_call | solution.py:384
  137.4 5.7 %collective-permute-done.2.b = bf16[192,2048]{1,0:T(8,128)(2,1)S(1)} collective-permute-done((bf16[192,2048]{1,0:T(8,128)(2,1)}, bf16[192,2048]{1,0:T(8,128)(2,1)S(1)}, u32[]{:S(2)}, u32[]{:S(2)}) %collective-permute-start.2) | collective-permute-done | bytes 786464 | tf_op jit(solution)/shard_map/ppermute | solution.py:460
  143.1 0.8 collective-permute-done.3.d
  143.9 0.0 copy-done.1
  144.0 0.0 copy-done.2
  144.0 0.4 shard_map.104
  144.3 2.5 %collective-permute-start.4 = (bf16[192,2048]{1,0:T(8,128)(2,1)S(1)}, bf16[192,2048]{1,0:T(8,128)(2,1)S(1)}, u32[]{:S(2)}, u32[]{:S(2)}) collective-permute-start(bf16[192,2048]{1,0:T(8,128)(2,1)S(1)} %get-tuple-element.45), channel_id=1, source_target_pairs={{0,6},{1,7},{2,0},{3,1},{4,2},{5,3},{6,4},{7,5},{8,14},{9,15},{10,... | collective-permute-start | bytes 2359304 | tf_op jit(solution)/shard_map/ppermute | solution.py:460
  146.9 0.0 collective-permute-start.5
  146.9 0.0 copy-done.7
  146.9 0.0 copy-start.5
  146.9 3.4 %copy-done.5 = f32[2048,1024]{1,0:T(8,128)S(1)} copy-done((f32[2048,1024]{1,0:T(8,128)S(1)}, f32[2048,1024]{1,0:T(8,128)}, u32[]{:S(2)}) %copy-start.5) | copy-done | bytes 8388632
  150.3 16.8 %shard_map.106 = (f32[2048,1024]{1,0:T(8,128)}, f32[1024,2048]{1,0:T(8,128)}) custom-call(bf16[3072,2048]{1,0:T(8,128)(2,1)} %get-tuple-element.48.a, bf16[3072,1024]{1,0:T(8,128)(2,1)S(1)} %copy-done.7, f32[2048,1024]{1,0:T(8,128)S(1)} %copy-done.5, f32[1024,2048]{1,0:T(8,128)} %get-tuple-element.51.refs_0_), custom_call_target="tpu_custom_call" | custom-call | flops 9663676416 | bytes 30932992 | tf_op jit(solution)/shard_map/pallas_call | solution.py:384
  167.0 0.0 collective-permute-done.near_a
  167.0 0.0 collective-permute-done.1.near_b
  167.0 0.0 collective-permute-done.4.far_a
  167.0 0.0 collective-permute-done.5.far_b
  167.0 0.0 copy-done
  167.1 0.0 copy-done.3
  167.1 0.0 copy-done.4
  167.1 2.1 %shard_map.105 = bf16[2,192,2048]{2,1,0:T(8,128)(2,1)} custom-call(bf16[2,192,2048]{2,1,0:T(8,128)(2,1)S(1)} %bitcast.2, bf16[64,2048]{1,0:T(8,128)(2,1)S(1)} %copy-done.3, bf16[64,2048]{1,0:T(8,128)(2,1)S(1)} %copy-done.4, bf16[128,2048]{1,0:T(8,128)(2,1)S(1)} %collective-permute-done.near_a, bf16[128,2048]{1,0:T(8,128)(2,1)S(1)} %collective-permute-done.1.near_b, ...), custom_call_target="tpu_custom_call" | custom-call | flops 2359296 | bytes 6291456 | tf_op jit(solution)/shard_map/pallas_call | solution.py:431
  (3 shorter events, 0.0 us)
Async XLA Ops:
  113.3 53.7 %collective-permute-start = (bf16[128,2048]{1,0:T(8,128)(2,1)}, bf16[128,2048]{1,0:T(8,128)(2,1)S(1)}, u32[]{:S(2)}, u32[]{:S(2)}) collective-permute-start(bf16[128,2048]{1,0:T(8,128)(2,1)} %get-tuple-element.32), channel_id=1, source_target_pairs={{0,2},{1,3},{2,4},{3,5},{4,6},{5,7},{6,0},{7,1},{8,10},{9,11},{10,... | collective-permute-start | bytes 1572872 | tf_op jit(solution)/shard_map/ppermute | solution.py:457
  114.2 52.9 %collective-permute-start.1 = (bf16[128,2048]{1,0:T(8,128)(2,1)}, bf16[128,2048]{1,0:T(8,128)(2,1)S(1)}, u32[]{:S(2)}, u32[]{:S(2)}) collective-permute-start(bf16[128,2048]{1,0:T(8,128)(2,1)} %get-tuple-element.33), channel_id=1, source_target_pairs={{0,6},{1,7},{2,0},{3,1},{4,2},{5,3},{6,4},{7,5},{8,14},{9,15},{10,... | collective-permute-start | bytes 1572872 | tf_op jit(solution)/shard_map/ppermute | solution.py:460
  116.1 27.0 %collective-permute-start.2 = (bf16[192,2048]{1,0:T(8,128)(2,1)}, bf16[192,2048]{1,0:T(8,128)(2,1)S(1)}, u32[]{:S(2)}, u32[]{:S(2)}) collective-permute-start(bf16[192,2048]{1,0:T(8,128)(2,1)} %get-tuple-element.35), channel_id=1, source_target_pairs={{0,6},{1,7},{2,0},{3,1},{4,2},{5,3},{6,4},{7,5},{8,14},{9,15},{10,... | collective-permute-start | bytes 2359304 | tf_op jit(solution)/shard_map/ppermute | solution.py:460
  116.7 27.3 %collective-permute-start.3 = (bf16[192,2048]{1,0:T(8,128)(2,1)}, bf16[192,2048]{1,0:T(8,128)(2,1)S(1)}, u32[]{:S(2)}, u32[]{:S(2)}) collective-permute-start(bf16[192,2048]{1,0:T(8,128)(2,1)} %get-tuple-element.36), channel_id=1, source_target_pairs={{0,2},{1,3},{2,4},{3,5},{4,6},{5,7},{6,0},{7,1},{8,10},{9,11},{10,... | collective-permute-start | bytes 2359304 | tf_op jit(solution)/shard_map/ppermute | solution.py:457
  117.6 3.4 %copy-start.6 = (f32[2048,1024]{1,0:T(8,128)S(1)}, f32[2048,1024]{1,0:T(8,128)}, u32[]{:S(2)}) copy-start(f32[2048,1024]{1,0:T(8,128)} %get-tuple-element.39.init) | copy-start | bytes 25165828
  120.9 2.8 %copy-start.8 = (bf16[3072,1024]{1,0:T(8,128)(2,1)S(1)}, bf16[3072,1024]{1,0:T(8,128)(2,1)}, u32[]{:S(2)}) copy-start(bf16[3072,1024]{1,0:T(8,128)(2,1)} %get-tuple-element.38.b) | copy-start | bytes 18874372
  123.7 20.2 %copy-start.1 = (bf16[192,2048]{1,0:T(8,128)(2,1)S(1)}, bf16[192,2048]{1,0:T(8,128)(2,1)}, u32[]{:S(2)}) copy-start(bf16[192,2048]{1,0:T(8,128)(2,1)} %get-tuple-element.34.a) | copy-start | bytes 2359300
  123.7 20.2 %copy-start.2 = (bf16[192,2048]{1,0:T(8,128)(2,1)S(1)}, bf16[192,2048]{1,0:T(8,128)(2,1)}, u32[]{:S(2)}) copy-start(bf16[192,2048]{1,0:T(8,128)(2,1)} %get-tuple-element.41.c) | copy-start | bytes 2359300
  123.7 23.1 %copy-start.7 = (bf16[3072,1024]{1,0:T(8,128)(2,1)S(1)}, bf16[3072,1024]{1,0:T(8,128)(2,1)}, u32[]{:S(2)}) copy-start(bf16[3072,1024]{1,0:T(8,128)(2,1)} %get-tuple-element.49.b) | copy-start | bytes 18874372
  144.3 22.7 %collective-permute-start.4 = (bf16[192,2048]{1,0:T(8,128)(2,1)S(1)}, bf16[192,2048]{1,0:T(8,128)(2,1)S(1)}, u32[]{:S(2)}, u32[]{:S(2)}) collective-permute-start(bf16[192,2048]{1,0:T(8,128)(2,1)S(1)} %get-tuple-element.45), channel_id=1, source_target_pairs={{0,6},{1,7},{2,0},{3,1},{4,2},{5,3},{6,4},{7,5},{8,14},{9,15},{10,... | collective-permute-start | bytes 2359304 | tf_op jit(solution)/shard_map/ppermute | solution.py:460
  146.9 20.2 %collective-permute-start.5 = (bf16[192,2048]{1,0:T(8,128)(2,1)S(1)}, bf16[192,2048]{1,0:T(8,128)(2,1)S(1)}, u32[]{:S(2)}, u32[]{:S(2)}) collective-permute-start(bf16[192,2048]{1,0:T(8,128)(2,1)S(1)} %get-tuple-element.46), channel_id=1, source_target_pairs={{0,2},{1,3},{2,4},{3,5},{4,6},{5,7},{6,0},{7,1},{8,10},{9,11},{10,... | collective-permute-start | bytes 2359304 | tf_op jit(solution)/shard_map/ppermute | solution.py:457
  146.9 3.4 %copy-start.5 = (f32[2048,1024]{1,0:T(8,128)S(1)}, f32[2048,1024]{1,0:T(8,128)}, u32[]{:S(2)}) copy-start(f32[2048,1024]{1,0:T(8,128)} %get-tuple-element.50.init) | copy-start | bytes 25165828
  150.2 16.8 %copy-start = (bf16[384,2048]{1,0:T(8,128)(2,1)S(1)}, bf16[384,2048]{1,0:T(8,128)(2,1)}, u32[]{:S(2)}) copy-start(bf16[384,2048]{1,0:T(8,128)(2,1)} %get-tuple-element.29) | copy-start | bytes 4718596
  150.2 16.8 %copy-start.3 = (bf16[64,2048]{1,0:T(8,128)(2,1)S(1)}, bf16[64,2048]{1,0:T(8,128)(2,1)}, u32[]{:S(2)}) copy-start(bf16[64,2048]{1,0:T(8,128)(2,1)} %get-tuple-element.30.got_a) | copy-start | bytes 786436
  150.3 16.8 %copy-start.4 = (bf16[64,2048]{1,0:T(8,128)(2,1)S(1)}, bf16[64,2048]{1,0:T(8,128)(2,1)}, u32[]{:S(2)}) copy-start(bf16[64,2048]{1,0:T(8,128)(2,1)} %get-tuple-element.31.got_b) | copy-start | bytes 786436
